TPU v7x, 32 devices: a whole 2x2x4 slice. The times are simulated.
32 devices in a mesh: dp: 2 (over x), tp: 16 (over z, y, core).
Axes of the slice: x: 2, y: 2, z: 4, core: 2. Of those that a mesh axis runs over, the one named last changes fastest.
Arguments:
- x_in: bfloat16 [6, 2048, 2560], P('dp'), parts along dimension 0
- seq_lens: int32 [6], P('dp'), parts along dimension 0
- ln1_gain: float32 [2560], replicated
- ln1_bias: float32 [2560], replicated
- w_qkv: bfloat16 [2560, 3, 32, 80], P(None, None, 'tp')
- b_qkv: bfloat16 [3, 32, 80], P(None, 'tp')
- w_out: bfloat16 [32, 80, 2560], P('tp')
- b_out: bfloat16 [2560], replicated
- ln2_gain: float32 [2560], replicated
- ln2_bias: float32 [2560], replicated
- w_up: bfloat16 [2560, 10240], P(None, 'tp')
- b_up: bfloat16 [10240], P('tp')
- w_down: bfloat16 [10240, 2560], P('tp')
- b_down: bfloat16 [2560], replicated
Outputs:
- output 1: bfloat16 [6, 2048, 2560], P('dp'), parts along dimension 0
- output 2: bfloat16 [6, 32, 2048, 80], P('dp', 'tp'), parts along dimension 0
- output 3: bfloat16 [6, 32, 2048, 80], P('dp', 'tp'), parts along dimension 0
There are 2 independent parts. A program takes and returns all parts, laid end to end along the dimension named above; an argument that names none is the same for every part.
All inputs are finite; a program needn't handle non-finite values.
Results may differ from a plain program's by a relative error of at most 0.0137091.
Values are sent between devices in bfloat16 or wider.
A program may use at most 1 GiB of HBM per device.

v0:
```python
import jax
import jax.numpy as jnp
from jax import lax
from jax.sharding import PartitionSpec as P


def layer_norm(values, gain_vec, bias_vec):
    values = values.astype(jnp.float32)
    row_mean = jnp.mean(values, axis=-1, keepdims=True)
    centered = values - row_mean
    row_var = jnp.mean(centered * centered, axis=-1, keepdims=True)
    return (centered * lax.rsqrt(row_var + 1e-5) * gain_vec + bias_vec).astype(jnp.bfloat16)


def cache_keep(values, seq_lens):
    positions = jnp.arange(values.shape[2])
    valid = positions[None, None, :, None] < seq_lens[:, None, None, None]
    return jnp.where(valid, values, 0)


def causal_mask(seq_lens, seq_len):
    positions = jnp.arange(seq_len)
    causal = positions[None, :] <= positions[:, None]
    in_length = positions[None, None, None, :] < seq_lens[:, None, None, None]
    return causal[None, None] & in_length


def attend(q_all, k_all, v_all, allowed):
    score_scale = q_all.shape[-1] ** -0.5
    scores = jnp.einsum("bhqk,bhsk->bhqs", q_all, k_all, preferred_element_type=jnp.float32) * score_scale
    scores = jnp.where(allowed, scores, -1e30)
    attn_probs = jax.nn.softmax(scores, axis=-1).astype(jnp.bfloat16)
    return jnp.einsum("bhqs,bhsk->bhqk", attn_probs, v_all, preferred_element_type=jnp.float32).astype(jnp.bfloat16)


def solution(mesh):
    def local_layer(x_in, seq_lens, ln1_gain, ln1_bias, w_qkv, b_qkv, w_out, b_out, ln2_gain, ln2_bias, w_up, b_up, w_down, b_down):
        normed = layer_norm(x_in, ln1_gain, ln1_bias)
        qkv_all = jnp.einsum("bsd,dthk->tbhsk", normed, w_qkv, preferred_element_type=jnp.float32)
        qkv_all = (qkv_all + b_qkv.astype(jnp.float32)[:, None, :, None, :]).astype(jnp.bfloat16)
        allowed = causal_mask(seq_lens, x_in.shape[1])
        attended = attend(qkv_all[0], qkv_all[1], qkv_all[2], allowed)
        part_out = jnp.einsum("cirl,ile->cre", attended, w_out, preferred_element_type=jnp.float32).astype(jnp.bfloat16)
        summed_out = lax.psum(part_out, "tp")
        x_mid = (x_in.astype(jnp.float32) + summed_out.astype(jnp.float32) + b_out.astype(jnp.float32)).astype(jnp.bfloat16)
        normed2 = layer_norm(x_mid, ln2_gain, ln2_bias)
        up_proj = jnp.einsum("bsd,df->bsf", normed2, w_up, preferred_element_type=jnp.float32) + b_up.astype(jnp.float32)
        hidden = jax.nn.relu(up_proj).astype(jnp.bfloat16)
        part_down = jnp.einsum("bsf,fd->bsd", hidden, w_down, preferred_element_type=jnp.float32).astype(jnp.bfloat16)
        summed_down = lax.psum(part_down, "tp")
        x_out = (x_mid.astype(jnp.float32) + summed_down.astype(jnp.float32) + b_down.astype(jnp.float32)).astype(jnp.bfloat16)
        return x_out, cache_keep(qkv_all[1], seq_lens), cache_keep(qkv_all[2], seq_lens)

    arg_specs = (P("dp", None, None), P("dp"), P(), P(), P(None, None, "tp", None), P(None, "tp", None), P("tp", None, None), P(), P(), P(), P(None, "tp"), P("tp"), P("tp", None), P())
    cache_spec = P("dp", "tp", None, None)
    result_specs = (P("dp", None, None), cache_spec, cache_spec)
    return jax.shard_map(local_layer, mesh=mesh, in_specs=arg_specs, out_specs=result_specs, check_vma=False)
```

profile of v0, /device:TPU:0, one launch (start us, length us, event | category | flops | bytes accessed | tf_op | source)
XLA Modules:
  0.0 1380.8 jit_solution(11228870672092588600)
XLA Ops:
  7.2 0.0 copy-start
  7.2 0.0 all-reduce.3.cloned.1.call-start
  7.2 2.1 iota_compare_fusion
  9.4 0.0 copy-start.7
  9.4 0.0 copy-start.8
  9.4 10.9 convert_reduce_fusion.1
  20.2 0.0 copy-start.10
  20.3 0.0 copy-start.11
  20.3 0.0 copy-start.12
  20.3 15.1 %fusion.10 = f32[3,2048]{1,0:T(4,128)S(1)} fusion(bf16[3,2048,2560]{2,1,0:T(8,128)(2,1)} %param.14, f32[3,2048]{1,0:T(4,128)S(1)} %broadcast_multiply_fusion.1), kind=kLoop, calls=%fused_computation.19 | loop fusion | flops 62908416 | bytes 31506432 | tf_op jit(solution)/shard_map/reduce_sum | solution.py:11
  35.4 0.0 copy-done.7
  35.4 0.0 copy-done.8
  35.4 0.1 iota_compare_fusion.1
  35.5 0.0 copy-start.2
  35.5 0.6 copy-done.2
  36.1 10.1 broadcast_and_fusion
  46.3 0.0 copy-done.10
  46.3 0.0 copy-done.11
  46.3 0.0 copy-done.12
  46.3 22.8 %fusion.39 = bf16[3,3,2,2048,80]{3,4,2,0,1:T(8,128)(2,1)} fusion(f32[3,2,80]{2,1,0:T(2,128)S(1)} %convert_element_type.64, bf16[3,2048,2560]{2,1,0:T(8,128)(2,1)} %param.14, f32[2560]{0:T(1024)S(1)} %copy-done.11, f32[2560]{0:T(1024)S(1)} %copy-done.12, f32[3,2048]{1,0:T(4,128)S(1)} %add_rsqrt_fusion.1, f32[3,2048]{1,0:T(4,128)S(1)} %broadcast_multiply_fusion.1, ...), kind=kOutput, calls=%fused_computation.47 | convolution fusion | flops 15199764480 | bytes 39884672 | tf_op jit(solution)/shard_map/bsd,dthk->tbhsk/dot_general | solution.py:39
  69.1 49.1 %fusion.53 = (f32[3,2,2048]{2,1,0:T(2,128)S(1)}, f32[3,2,2048,2048]{2,3,1,0:T(8,128)}) fusion(pred[3,2048,2048]{1,2,0:T(8,128)(4,1)} %broadcast_and_fusion, bf16[3,3,2,2048,80]{3,4,2,0,1:T(8,128)(2,1)} %fusion.39), kind=kOutput, calls=%fused_computation.67 | convolution fusion | flops 4127197184 | bytes 117227520 | tf_op jit(solution)/shard_map/sub | solution.py:32
  118.2 0.0 copy-start.1
  118.2 32.7 %fusion.45 = bf16[3,2,2048,80]{2,3,1,0:T(8,128)(2,1)S(1)} fusion(f32[3,2,2048,2048]{2,3,1,0:T(8,128)} %get-tuple-element.8, f32[3,2,2048]{2,1,0:T(2,128)S(1)} %get-tuple-element.7, bf16[3,3,2,2048,80]{3,4,2,0,1:T(8,128)(2,1)} %fusion.39), kind=kOutput, calls=%fused_computation.50 | convolution fusion | flops 4077846528 | bytes 104644608 | tf_op jit(solution)/shard_map/bhqs,bhsk->bhqk/dot_general | solution.py:33
  151.0 0.0 copy-done.1
  151.0 0.0 copy-start.4
  151.0 0.0 copy-start.6
  151.0 14.1 %bitcast_convert_fusion = bf16[3,2048,2560]{2,1,0:T(8,128)(2,1)} fusion(bf16[3,2,2048,80]{2,3,1,0:T(8,128)(2,1)S(1)} %fusion.45, bf16[2,80,2560]{2,1,0:T(8,128)(2,1)S(1)} %copy-done.1), kind=kOutput, calls=%fused_computation.27 | convolution fusion | flops 5048893440 | bytes 34242560 | tf_op jit(solution)/shard_map/cirl,ile->cre/dot_general | solution.py:43
  165.1 0.0 all-reduce.3.cloned.1.call-update
  165.1 0.0 all-reduce.5.cloned.1.call-start
  165.2 0.0 copy-done.4
  165.2 0.0 copy-done.6
  165.2 535.1 %all-reduce.3.cloned.1.call-done = bf16[3,2048,2560]{2,1,0:T(8,128)(2,1)} async-done(((bf16[3,2048,2560]{2,1,0:T(8,128)(2,1)}), bf16[3,2048,2560]{2,1,0:T(8,128)(2,1)}) %all-reduce.3.cloned.1.call-update) | async-done | bytes 31457296 | tf_op jit(solution)/shard_map/psum | solution.py:44
  700.3 31.6 %convert_reduce_fusion = (f32[3,2048]{1,0:T(4,128)S(1)}, bf16[3,2048,2560]{2,1,0:T(8,128)(2,1)}) fusion(f32[2560]{0:T(1024)S(1)} %convert_element_type.71, bf16[3,2048,2560]{2,1,0:T(8,128)(2,1)} %all-reduce.3.cloned.1.call-done, bf16[3,2048,2560]{2,1,0:T(8,128)(2,1)} %param.14), kind=kLoop, calls=%fused_computation.6 | loop fusion | flops 110094336 | bytes 94406656 | tf_op jit(solution)/shard_map/reduce_sum | solution.py:9
  731.9 0.0 copy-start.9
  731.9 0.0 copy-start.13
  731.9 0.0 copy-start.14
  732.0 15.1 %fusion.6 = f32[3,2048]{1,0:T(4,128)S(1)} fusion(bf16[3,2048,2560]{2,1,0:T(8,128)(2,1)} %get-tuple-element.4, f32[3,2048]{1,0:T(4,128)S(1)} %broadcast_multiply_fusion), kind=kLoop, calls=%fused_computation.15 | loop fusion | flops 62908416 | bytes 31506432 | tf_op jit(solution)/shard_map/reduce_sum | solution.py:11
  747.1 0.0 copy-done.9
  747.1 0.0 copy-done.13
  747.1 0.0 copy-done.14
  747.1 30.9 %maximum_convert_fusion.4 = bf16[3,2048,640]{2,1,0:T(8,128)(2,1)} fusion(bf16[3,2048,2560]{2,1,0:T(8,128)(2,1)} %get-tuple-element.4, f32[2560]{0:T(1024)S(1)} %copy-done.13, f32[2560]{0:T(1024)S(1)} %copy-done.14, f32[3,2048]{1,0:T(4,128)S(1)} %add_rsqrt_fusion, f32[3,2048]{1,0:T(4,128)S(1)} %broadcast_multiply_fusion, ...), kind=kOutput, calls=%fused_computation.42.clone.clone.1 | convolution fusion | flops 20238827520 | bytes 42670592 | tf_op jit(solution)/shard_map/bsd,df->bsf/dot_general | solution.py:47
  778.0 31.5 %convolution_convert_fusion = bf16[3,2048,2560]{2,1,0:T(8,128)(2,1)} fusion(bf16[640,2560]{1,0:T(8,128)(2,1)S(1)} %copy-done, bf16[3,2048,640]{2,1,0:T(8,128)(2,1)} %maximum_convert_fusion.4), kind=kOutput, calls=%fused_computation.40 | convolution fusion | flops 20148387840 | bytes 42598400 | tf_op jit(solution)/shard_map/bsf,fd->bsd/dot_general | solution.py:49
  809.5 0.0 all-reduce.5.cloned.1.call-update
  809.5 0.7 copy-done.5
  810.1 0.0 copy-done.3
  810.2 4.3 broadcast_select_fusion
  814.5 527.2 %all-reduce.5.cloned.1.call-done = bf16[3,2048,2560]{2,1,0:T(8,128)(2,1)} async-done(((bf16[3,2048,2560]{2,1,0:T(8,128)(2,1)}), bf16[3,2048,2560]{2,1,0:T(8,128)(2,1)}) %all-reduce.5.cloned.1.call-update) | async-done | bytes 31457296 | tf_op jit(solution)/shard_map/psum | solution.py:50
  1341.7 32.2 %fusion.17 = bf16[3,2048,2560]{2,1,0:T(8,128)(2,1)} fusion(bf16[3,2048,2560]{2,1,0:T(8,128)(2,1)} %get-tuple-element.4, bf16[3,2048,2560]{2,1,0:T(8,128)(2,1)} %all-reduce.5.cloned.1.call-done, f32[2560]{0:T(1024)S(1)} %convert_element_type.79), kind=kLoop, calls=%fused_computation.26 | loop fusion | flops 78643200 | bytes 94382080 | tf_op jit(solution)/shard_map/convert_element_type | solution.py:51
  (11 shorter events, 0.1 us)
Async XLA Ops:
  7.2 770.8 %copy-start = (bf16[640,2560]{1,0:T(8,128)(2,1)S(1)}, bf16[640,2560]{1,0:T(8,128)(2,1)}, u32[]{:S(2)}) copy-start(bf16[640,2560]{1,0:T(8,128)(2,1)} %param.26) | copy-start | bytes 9830404
  7.2 693.1 %all-reduce.3.cloned.1.call-start = ((), (), s32[]{:S(2)}) async-start(), calls=%async_computation | async-start | bytes 62914560 | tf_op jit(solution)/shard_map/psum | solution.py:44
  9.4 26.1 %copy-start.7 = (bf16[3,2,80]{2,1,0:T(2,128)(2,1)S(1)}, bf16[3,2,80]{2,1,0:T(2,128)(2,1)}, u32[]{:S(2)}) copy-start(bf16[3,2,80]{2,1,0:T(2,128)(2,1)} %param.19) | copy-start | bytes 2884
  9.4 26.1 %copy-start.8 = (s32[3]{0:T(128)S(1)}, s32[3]{0:T(128)}, u32[]{:S(2)}) copy-start(s32[3]{0:T(128)} %param.15) | copy-start | bytes 40
  20.2 26.0 %copy-start.10 = (bf16[2560,3,2,80]{0,3,2,1:T(8,128)(2,1)S(1)}, bf16[2560,3,2,80]{0,3,2,1:T(8,128)(2,1)}, u32[]{:S(2)}) copy-start(bf16[2560,3,2,80]{0,3,2,1:T(8,128)(2,1)} %param.18) | copy-start | bytes 7372804
  20.3 26.0 %copy-start.11 = (f32[2560]{0:T(1024)S(1)}, f32[2560]{0:T(1024)}, u32[]{:S(2)}) copy-start(f32[2560]{0:T(1024)} %param.17) | copy-start | bytes 30724
  20.3 26.0 %copy-start.12 = (f32[2560]{0:T(1024)S(1)}, f32[2560]{0:T(1024)}, u32[]{:S(2)}) copy-start(f32[2560]{0:T(1024)} %param.16) | copy-start | bytes 30724
  35.5 0.6 copy-start.2
  118.2 32.7 %copy-start.1 = (bf16[2,80,2560]{2,1,0:T(8,128)(2,1)S(1)}, bf16[2,80,2560]{2,1,0:T(8,128)(2,1)}, u32[]{:S(2)}) copy-start(bf16[2,80,2560]{2,1,0:T(8,128)(2,1)} %param.20) | copy-start | bytes 2457604
  151.0 14.2 %copy-start.4 = (bf16[2560]{0:T(1024)(128)(2,1)S(1)}, bf16[2560]{0:T(1024)(128)(2,1)}, u32[]{:S(2)}) copy-start(bf16[2560]{0:T(1024)(128)(2,1)} %param.21) | copy-start | bytes 15364
  151.0 14.2 %copy-start.6 = (bf16[640]{0:T(1024)(128)(2,1)S(1)}, bf16[640]{0:T(1024)(128)(2,1)}, u32[]{:S(2)}) copy-start(bf16[640]{0:T(1024)(128)(2,1)} %param.25) | copy-start | bytes 3844
  165.1 1176.6 %all-reduce.5.cloned.1.call-start = ((), (), s32[]{:S(2)}) async-start(), calls=%async_computation.1 | async-start | bytes 62914560 | tf_op jit(solution)/shard_map/psum | solution.py:50
  731.9 15.2 %copy-start.9 = (bf16[2560,640]{1,0:T(8,128)(2,1)S(1)}, bf16[2560,640]{1,0:T(8,128)(2,1)}, u32[]{:S(2)}) copy-start(bf16[2560,640]{1,0:T(8,128)(2,1)} %param.24) | copy-start | bytes 9830404
  731.9 15.2 %copy-start.13 = (f32[2560]{0:T(1024)S(1)}, f32[2560]{0:T(1024)}, u32[]{:S(2)}) copy-start(f32[2560]{0:T(1024)} %param.23) | copy-start | bytes 30724
  731.9 15.2 %copy-start.14 = (f32[2560]{0:T(1024)S(1)}, f32[2560]{0:T(1024)}, u32[]{:S(2)}) copy-start(f32[2560]{0:T(1024)} %param.22) | copy-start | bytes 30724
  809.5 0.7 copy-start.5
  809.5 0.7 copy-start.3
Sparse Core Ops, SparseCore 0:
  165.2 535.0 all-reduce.2
  809.6 532.0 all-reduce.4
where the time goes:
time: 1380 us
  waiting for transfers between devices  1060 us (77%)
  matrix products  181 us (13%)
  other arithmetic  122 us (9%)
  between operations  14.3 us (1%)
    psum x1, waiting for transfers between devices, local_layer(): summed_out = lax.psum(part_out, 'tp')  535 us
    psum x1, waiting for transfers between devices, local_layer(): summed_down = lax.psum(part_down, 'tp')  527 us
    sub x1, matrix products, attend(): attn_probs = jax.nn.softmax(scores, axis=-1).astype(jnp.bfloat16)  49.1 us
    reduce_sum x2, other arithmetic, layer_norm(): row_mean = jnp.mean(values, axis=-1, keepdims=True)  42.4 us
    dot_general x1, matrix products, attend(): jnp.einsum('bhqs,bhsk->bhqk', attn_probs, v_all, preferred_element_type=j...  32.7 us
    convert_element_type x1, other arithmetic, local_layer(): (x_mid.astype(jnp.float32) + summed_down.astype(jnp.float32) + b_down.ast...  32.2 us
    dot_general x1, matrix products, local_layer(): jnp.einsum('bsf,fd->bsd', hidden, w_down, preferred_element_type=jnp.floa...  31.5 us
    dot_general x1, matrix products, local_layer(): jnp.einsum('bsd,df->bsf', normed2, w_up, preferred_element_type=jnp.float32)  30.9 us
  transfers between devices with their start and end apart: 2, of which 2 were waited for; matrix products, arithmetic and copies ran while one was open for 0% of the time, Pallas kernels for 0%

commit v1 on v0

v1 whole, which is shorter than its diff:
```python
import functools

import jax
import jax.numpy as jnp
from jax import lax
from jax.experimental import pallas as pl
from jax.experimental.pallas import tpu as pltpu
from jax.sharding import PartitionSpec as P

D, S, HD, FF = 2560, 2048, 80, 640
BF = jnp.bfloat16
MESH = pl.DeviceIdType.MESH
ANY = pl.BlockSpec(memory_space=pl.ANY)
NT = (((1,), (1,)), ((), ()))
TN = (((0,), (0,)), ((), ()))
SCALE = HD ** -0.5
LOG2E = 1.4426950408889634


def ln_rows(x, gain, bias):
    centered = x - jnp.mean(x, axis=-1, keepdims=True)
    var = jnp.mean(centered * centered, axis=-1, keepdims=True)
    return (centered * lax.rsqrt(var + 1e-5) * gain + bias).astype(BF)


TB, KA, NS = 256, 96, 3
QB = S // 4
PER_SEQ = S // TB
UC = 2
CHUNKS = tuple((s, h) for s in range(NS) for h in range(2))


def front_kernel(lens_ref, x_ref, vec_ref, wq_ref, bq_ref, wo_ref, wup_ref, bup_ref, wdn_ref,
                 k_out, v_out, x1_out, u_out, dn_out,
                 wt, wu, a_all, xb, q_s, k_s, v_s, kt, a_st, bu, st1, st2,
                 xsem, csem, osem, lsem, wsem, wos, wor, wol, woy_s, woy_r, wod_s, wod_r, ay_s, ay_r, as_, ar, al, ad_s, ad_r,
                 b_s, b_r, yu_s, yu_r, yd_s, yd_r, xu_s, xu_r, xd_s, xd_r):
    group, me = lax.axis_index("dp"), lax.axis_index("tp")
    z, y, c = me // 4, (me // 2) % 2, me % 2
    dev = lambda z_, y_, c_: (group, z_ * 4 + y_ * 2 + c_)
    partner, ypeer, across = dev(z, y, 1 - c), dev(z, 1 - y, c), (1 - group, me)
    right, left = dev((z + 1) % 4, y, c), dev((z + 3) % 4, y, c)
    ln1_gain, ln1_bias, b_out, ln2_gain, ln2_bias = (vec_ref[i:i + 1] for i in range(5))
    sent = []

    def remote(src, dst, ss, rs, to):
        return pltpu.make_async_remote_copy(src, dst, ss, rs, device_id=to, device_id_type=MESH)

    def go(copy, when=None):
        if when is None:
            copy.start()
        else:
            @pl.when(when)
            def _():
                copy.start()
        sent.append((copy, when))

    place = lambda z_, y_, c_: (z_ * 2 + c_) * 2 + y_
    mine = place(z, y, c)
    wo_rows = lambda z_, y_: wt.at[pl.ds(pl.multiple_of(place(z_, y_, c) * 2 * HD, 32), 2 * HD)]

    def wo_line(k, to_right):
        z_ = (z + 4 - k) % 4 if to_right else (z + k) % 4
        rows = wo_rows(z_, y)
        i = k + 3 * (not to_right)
        return remote(wo_ref if k == 0 else rows, rows, wos.at[i], (wor if to_right else wol).at[k], right if to_right else left)

    def wo_y(z_, own=False):
        rows = wo_rows(z_, y)
        return remote(wo_ref if own else rows, rows, woy_s.at[z_], woy_r.at[z_], ypeer)

    def wo_core(z_, y_, own=False):
        rows = wo_rows(z_, y_)
        return remote(wo_ref if own else rows, rows, wod_s, wod_r, partner)

    def a_y(i):
        s, h = CHUNKS[i]
        return remote(a_st.at[s, 2 * (1 - y) + h], a_all.at[s, h, mine], ay_s.at[i], ay_r.at[i], ypeer)

    def a_line(i, k, to_right):
        s, h = CHUNKS[i]
        z_ = (z + 4 - k) % 4 if to_right else (z + k) % 4
        pair = a_all.at[s, h, pl.ds(place(z_, 0, c), 2)]
        return remote(pair, pair, as_.at[i * 6 + k + 3 * (not to_right)], (ar if to_right else al).at[i * 3 + k], right if to_right else left)

    def a_core(i, z_):
        s, h = CHUNKS[i]
        pair = a_all.at[s, h, pl.ds(place(z_, 0, c), 2)]
        return remote(pair, pair, ad_s.at[i], ad_r.at[i], partner)

    hu, hd = D // 2, FF // 2
    cu, cd = hu // UC, hd // UC

    def up_rows(n):
        return pl.ds(pl.multiple_of(group * hu + n * cu, 32), cu)

    def dn_rows(n):
        return pl.ds(pl.multiple_of(group * hd + n * cd, 32), cd)

    def yu(n):
        return remote(wup_ref.at[up_rows(n)], wu.at[1, up_rows(n)], yu_s.at[n], yu_r.at[n], ypeer)

    def xu(n):
        return remote(wu.at[1, up_rows(n)], wu.at[1, up_rows(n)], xu_s.at[n], xu_r.at[n], across)

    def yd(n):
        return remote(wdn_ref.at[dn_rows(n)], dn_out.at[dn_rows(n)], yd_s.at[n], yd_r.at[n], ypeer)

    def xd(n):
        return remote(dn_out.at[dn_rows(n)], dn_out.at[dn_rows(n)], xd_s.at[n], xd_r.at[n], across)

    bias_flow = remote(bup_ref, bu.at[1], b_s, b_r, ypeer)

    def hop(line, k, then):
        @pl.when(z >= k + 1)
        def _():
            line(k, True).wait_recv()

        if k < 2:
            go(line(k + 1, True), (z >= k + 1) & (z < 3))
        then((z + 3 - k) % 4, z >= k + 1)

        @pl.when(z <= 2 - k)
        def _():
            line(k, False).wait_recv()

        if k < 2:
            go(line(k + 1, False), (z <= 2 - k) & (z > 0))
        then((z + 1 + k) % 4, z <= 2 - k)

    def begin(line):
        go(line(0, True), z < 3)
        go(line(0, False), z > 0)

    def start_if(copy, when):
        @pl.when(when)
        def _():
            copy.start()

    def wo_then(z_, when):
        start_if(wo_y(z_), when)
        start_if(wo_core(z_, y), when)

    def wo_hop(k):
        hop(wo_line, k, wo_then)

    def wo_from_y():
        for z_ in range(4):
            wo_y(z_).wait_recv()
            wo_core(z_, 1 - y).start()

    def a_begin(s):
        for i in (2 * s, 2 * s + 1):
            a_y(i).wait_recv()
            begin(functools.partial(a_line, i))
            a_core(i, z).start()

    def a_hop(s, k):
        for i in (2 * s, 2 * s + 1):
            hop(functools.partial(a_line, i), k, lambda z_, when: start_if(a_core(i, z_), when))

    barrier = pltpu.get_barrier_semaphore()
    peers = (partner, ypeer, across, right, left)
    for p in peers:
        pl.semaphore_signal(barrier, inc=1, device_id=p, device_id_type=MESH)

    def x_copy(g):
        return pltpu.make_async_copy(x_ref.at[g // PER_SEQ, pl.ds(pl.multiple_of((g % PER_SEQ) * TB, TB), TB)], xb.at[g % 2], xsem.at[g % 2])

    x_copy(0).start()
    locals_ = [pltpu.make_async_copy(wo_ref, wo_rows(z, y), wsem.at[0]), pltpu.make_async_copy(bup_ref, bu.at[0], wsem.at[1]), pltpu.make_async_copy(wup_ref, wu.at[0], wsem.at[2])]
    for copy in locals_:
        copy.start()
    row = lax.broadcasted_iota(jnp.int32, (KA - HD, S), 0)
    for h in range(2):
        q_s[h, HD:] = jnp.where(row == 0, 1.0, 0.0).astype(BF)
    pl.semaphore_wait(barrier, len(peers))

    begin(wo_line)
    wo_y(z, True).start()
    wo_core(z, y, True).start()
    go(bias_flow)

    def qkv(s):
        n = lens_ref[s]

        @pl.loop(0, PER_SEQ)
        def _(b):
            g = s * PER_SEQ + b
            x_copy(g).wait()

            @pl.when(g + 1 < NS * PER_SEQ)
            def _():
                x_copy(g + 1).start()

            h = ln_rows(xb[g % 2].astype(jnp.float32), ln1_gain, ln1_bias)
            t = lax.dot_general(wq_ref[...], h, NT, preferred_element_type=jnp.float32)
            t = (t + bq_ref[...]).astype(BF)
            cols = pl.ds(pl.multiple_of(b * TB, TB), TB)
            keep = b * TB + lax.broadcasted_iota(jnp.int32, (1, TB), 1) < n
            for i in range(2):
                q_s[i, :HD, cols] = t[i * HD:(i + 1) * HD]
                k_s[i, :HD, cols] = jnp.where(keep, t[(2 + i) * HD:(3 + i) * HD], 0)
                v_s[i, :, cols] = jnp.where(keep, t[(4 + i) * HD:(5 + i) * HD], 0)

        pos = lax.broadcasted_iota(jnp.int32, (KA - HD, S), 1)
        for i in range(2):
            k_s[i, HD:] = jnp.where((row == 0) & (pos >= n), -1e30, 0.0).astype(BF)
            kt[i] = k_s[i].T
        for copy in caches(s):
            copy.start()

    def caches(s):
        return [pltpu.make_async_copy(k_s.at[:, pl.ds(0, HD)], k_out.at[s], csem.at[0]), pltpu.make_async_copy(v_s, v_out.at[s], csem.at[1])]

    def attend(s):
        causal = lax.broadcasted_iota(jnp.int32, (QB, QB), 0) <= lax.broadcasted_iota(jnp.int32, (QB, QB), 1)

        @pl.loop(0, 4)
        def _(t):
            at_q = pl.ds(pl.multiple_of(t * QB, QB), QB)

            def block(h, j, m, l, acc, masked):
                at = pl.ds(pl.multiple_of(j * QB, QB), QB)
                sc = jnp.dot(kt[h, at], q_s[h, :, at_q], preferred_element_type=jnp.float32) * (SCALE * LOG2E)
                if masked:
                    sc = jnp.where(causal, sc, -1e30)
                m_new = jnp.maximum(m, jnp.max(sc, axis=0, keepdims=True))
                p = jnp.exp2(sc - m_new)
                scale = jnp.exp2(m - m_new)
                l = scale * l + jnp.sum(p, axis=0, keepdims=True)
                acc = scale * acc + jnp.dot(v_s[h, :, at], p.astype(BF), preferred_element_type=jnp.float32)
                return m_new, l, acc

            zero = (jnp.full((1, QB), -1e30, jnp.float32), jnp.zeros((1, QB), jnp.float32), jnp.zeros((HD, QB), jnp.float32))
            carry = lax.fori_loop(0, t, lambda j, c: tuple(block(h, j, *c[h], False) for h in range(2)), (zero, zero))
            for h in range(2):
                _, l, acc = block(h, t, *carry[h], True)
                a_st[s, t, h * HD:(h + 1) * HD] = (acc / l).astype(BF)

            @pl.when(t // 2 == y)
            def _():
                a_all[s, t % 2, mine] = a_st[s, t]

        for copy in caches(s):
            copy.wait()
        go(a_y(2 * s))
        go(a_y(2 * s + 1))

    per = QB // TB
    n_blocks = NS * 2 * per

    def res_copy(i):
        rows = pl.ds(pl.multiple_of(y * (S // 2) + (i % (2 * per)) * TB, TB), TB)
        return pltpu.make_async_copy(x_ref.at[i // (2 * per), rows], xb.at[i % 2], xsem.at[i % 2])

    def put_x1(i):
        return pltpu.make_async_copy(st1.at[i % 2], x1_out.at[pl.ds(pl.multiple_of(i * TB, TB), TB)], osem.at[i % 2])

    def put_u(i):
        return pltpu.make_async_copy(st2.at[i % 2], u_out.at[pl.ds(pl.multiple_of(i * TB, TB), TB)], lsem.at[i % 2])

    def middle(i):
        s, h = CHUNKS[i]
        whole = a_all.at[s, h, pl.ds(0, 8)]
        pltpu.make_async_copy(whole, whole, ad_r.at[i]).wait()

        @pl.loop(i * per, (i + 1) * per)
        def _(b):
            res_copy(b).wait()

            @pl.when(b + 1 < n_blocks)
            def _():
                res_copy(b + 1).start()

            a = a_all[s, h, :, :, pl.ds(pl.multiple_of((b % per) * TB, TB), TB)].reshape(D, TB)
            o = lax.dot_general(a, wt[...], TN, preferred_element_type=jnp.float32)
            x1 = (xb[b % 2].astype(jnp.float32) + o + b_out).astype(BF)

            @pl.when(b >= 2)
            def _():
                put_x1(b - 2).wait()
                put_u(b - 2).wait()

            st1[b % 2] = x1
            put_x1(b).start()
            hid = ln_rows(x1.astype(jnp.float32), ln2_gain, ln2_bias)
            for n in range(2):
                up = jnp.dot(hid, wu[n], preferred_element_type=jnp.float32) + bu[n, 0:1]
                st2[b % 2, :, n * FF:(n + 1) * FF] = jnp.maximum(up, 0).astype(BF)
            put_u(b).start()

    qkv(0)
    wo_hop(0)
    attend(0)
    wo_hop(1)
    go(yu(0))
    qkv(1)
    a_begin(0)
    wo_hop(2)
    attend(1)
    go(yu(1))
    a_hop(0, 0)
    wo_from_y()
    qkv(2)
    a_hop(0, 1)
    a_begin(1)
    attend(2)
    res_copy(0).start()
    for n in range(UC):
        go(yd(n))
    for n in range(UC):
        yu(n).wait_recv()
        go(xu(n))
    a_hop(0, 2)
    a_hop(1, 0)
    whole = wt.at[pl.ds(0, D // 2)]
    pltpu.make_async_copy(whole, whole, wod_r).wait()
    bias_flow.wait_recv()
    for copy in locals_:
        copy.wait()
    a_begin(2)
    a_hop(1, 1)
    for n in range(UC):
        xu(n).wait_recv()
    middle(0)
    a_hop(2, 0)
    a_hop(1, 2)
    for n in range(UC):
        yd(n).wait_recv()
        go(xd(n))
    middle(1)
    a_hop(2, 1)
    middle(2)
    a_hop(2, 2)
    middle(3)
    middle(4)
    middle(5)
    for n in range(UC):
        xd(n).wait_recv()
    for b in range(n_blocks - 2, n_blocks):
        put_x1(b).wait()
        put_u(b).wait()
    for copy, when in sent:
        if when is None:
            copy.wait_send()
        else:
            @pl.when(when)
            def _():
                copy.wait_send()
    for z_ in range(4):
        wo_y(z_).wait_send()
    pltpu.make_async_copy(whole, whole, wod_s).wait()
    for i, (s, h) in enumerate(CHUNKS):
        pairs = a_all.at[s, h, pl.ds(0, 8)]
        pltpu.make_async_copy(pairs, pairs, ad_s.at[i]).wait()


def front(lens, x, vec, wq, bq, wo, wup, bup, wdn):
    v = pl.BlockSpec(memory_space=pltpu.VMEM)
    sem = lambda n: pltpu.SemaphoreType.DMA((n,))
    one = pltpu.SemaphoreType.DMA
    cache = jax.ShapeDtypeStruct((NS, 2, HD, S), BF)
    rows = lambda n: jax.ShapeDtypeStruct((NS * S // 2, n), BF)
    nc = len(CHUNKS)
    return pl.pallas_call(
        front_kernel,
        out_shape=(cache, cache, rows(D), rows(2 * FF), jax.ShapeDtypeStruct((FF, D), BF)),
        in_specs=[pl.BlockSpec(memory_space=pltpu.SMEM), ANY, v, v, v, ANY, ANY, ANY, ANY],
        out_specs=(ANY,) * 5,
        scratch_shapes=[
            pltpu.VMEM((D, D), BF), pltpu.VMEM((2, D, FF), BF), pltpu.VMEM((NS, 2, 16, 2 * HD, QB), BF), pltpu.VMEM((2, TB, D), BF),
            pltpu.VMEM((2, KA, S), BF), pltpu.VMEM((2, KA, S), BF), pltpu.VMEM((2, HD, S), BF), pltpu.VMEM((2, S, KA), BF),
            pltpu.VMEM((NS, 4, 2 * HD, QB), BF), pltpu.VMEM((2, 8, FF), jnp.float32), pltpu.VMEM((2, TB, D), BF), pltpu.VMEM((2, TB, 2 * FF), BF),
            sem(2), sem(2), sem(2), sem(2), sem(3), sem(6), sem(3), sem(3), sem(4), sem(4), one, one, sem(nc), sem(nc), sem(6 * nc), sem(3 * nc), sem(3 * nc), sem(nc), sem(nc),
            one, one, sem(UC), sem(UC), sem(UC), sem(UC), sem(UC), sem(UC), sem(UC), sem(UC),
        ],
        compiler_params=pltpu.CompilerParams(collective_id=1, has_side_effects=True, vmem_limit_bytes=63 * 2**20),
        cost_estimate=pl.CostEstimate(flops=10**11, bytes_accessed=10**8, transcendentals=0),
        name="front",
    )(lens, x, vec, wq, bq, wo, wup, bup, wdn)


BR = 128
NB = 3 * S // 2 // BR
Q = BR // 8
CH = BR // 2
SLOTS, S1N = 6, 4


def down_kernel(u_ref, w0_ref, w1_ref, x1_ref, bd_ref, o_ref,
                wd, ub, x1b, pt, acc, s1, r1, sm, rr, rl, fin,
                wsem, usem, xsem, lsem, s1s, r1s, sms, rrs, rls, zs, frs, fls, ys, yr, ds, dr):
    group, me = lax.axis_index("dp"), lax.axis_index("tp")
    z, y, c = me // 4, (me // 2) % 2, me % 2
    dev = lambda z_, y_, c_: (group, z_ * 4 + y_ * 2 + c_)
    partner, ypeer = dev(z, y, 1 - c), dev(z, 1 - y, c)
    right, left = dev((z + 1) % 4, y, c), dev((z + 3) % 4, y, c)

    barrier = pltpu.get_barrier_semaphore()
    for peer in (partner, ypeer, right, left):
        pl.semaphore_signal(barrier, inc=1, device_id=peer, device_id_type=MESH)

    loads = [pltpu.make_async_copy(w, wd.at[pl.ds(i * FF, FF)], wsem.at[i]) for i, w in enumerate((w0_ref, w1_ref))]
    for copy in loads:
        copy.start()

    def u_load(b):
        return pltpu.make_async_copy(u_ref.at[pl.ds(pl.multiple_of(b * BR, BR), BR)], ub.at[b], usem.at[b])

    def x1_load(b):
        rows = pl.ds(pl.multiple_of(b * BR + c * CH + z * Q, Q), Q)
        return pltpu.make_async_copy(x1_ref.at[rows], x1b.at[b], xsem.at[b])

    @pl.loop(0, NB)
    def _(b):
        u_load(b).start()
        x1_load(b).start()

    for copy in loads:
        copy.wait()
    pl.semaphore_wait(barrier, 4)

    per = NB // 3

    def rows_of(b, z_, y_):
        pos = (S // 2) * y_ + BR * (b % per) + CH * c + Q * z_
        return pl.ds(pl.multiple_of((b // per) * S + pos, Q), Q)

    def remote(src, dst, ss, rs, to):
        return pltpu.make_async_remote_copy(src, dst, ss, rs, device_id=to, device_id_type=MESH)

    def swap(b):
        return remote(s1.at[b % S1N], r1.at[b], s1s.at[b % S1N], r1s.at[b], partner)

    def chain(b, n, at, to_right):
        dst, sem = (rr, rrs) if to_right else (rl, rls)
        return remote(sm.at[b, pl.ds(at, n * Q)], dst.at[b, pl.ds(0, n * Q)], sms, sem.at[b], right if to_right else left)

    def go_right(b, k):
        rows = rows_of(b, (z + 4 - k) % 4, y)
        return remote(fin.at[b] if k == 0 else o_ref.at[rows], o_ref.at[rows], zs, frs.at[b * 3 + k], right)

    def go_left(b, k):
        rows = rows_of(b, (z + k) % 4, y)
        return remote(fin.at[b] if k == 0 else o_ref.at[rows], o_ref.at[rows], zs, fls.at[b * 3 + k], left)

    def go_y(b, z_, own=False):
        rows = rows_of(b, z_, y)
        return remote(fin.at[b] if own else o_ref.at[rows], o_ref.at[rows], ys, yr.at[b * 4 + z_], ypeer)

    def go_core(b, z_, y_, own=False):
        rows = rows_of(b, z_, y_)
        return remote(fin.at[b] if own else o_ref.at[rows], o_ref.at[rows], ds, dr, partner)

    f32 = lambda v: v.astype(jnp.float32)

    def multiply(b):
        u_load(b).wait()

        @pl.when(b >= S1N)
        def _():
            swap(b - S1N).wait_send()

        @pl.loop(0, 5)
        def _(j):
            cols = pl.ds(pl.multiple_of(j * 512, 512), 512)
            pt[...] = jnp.dot(ub[b], wd[:, cols], preferred_element_type=jnp.float32)
            acc[b % SLOTS, :, cols] = pt[pl.ds(pl.multiple_of(c * CH, CH), CH)]
            s1[b % S1N, :, cols] = pt[pl.ds(pl.multiple_of((1 - c) * CH, CH), CH)].astype(BF)

        swap(b).start()

    def own(i, n=1):
        return slice(i * Q, (i + n) * Q)

    def stage2(b):
        swap(b).wait_recv()
        acc[b % SLOTS] += f32(r1[b])

        @pl.when(z == 0)
        def _():
            sm[b] = acc[b % SLOTS, own(1, 3)].astype(BF)
            chain(b, 3, 0, True).start()

        @pl.when(z == 3)
        def _():
            sm[b] = acc[b % SLOTS, own(0, 3)].astype(BF)
            chain(b, 3, 0, False).start()

    def stage3(b):
        a = acc.at[b % SLOTS]

        @pl.when(z == 1)
        def _():
            chain(b, 3, 0, True).wait_recv()
            a[own(1)] += f32(rr[b, own(0)])
            sm[b, own(0, 2)] = (a[own(2, 2)] + f32(rr[b, own(1, 2)])).astype(BF)
            chain(b, 2, 0, True).start()

        @pl.when(z == 2)
        def _():
            chain(b, 3, 0, False).wait_recv()
            a[own(2)] += f32(rl[b, own(2)])
            sm[b, own(0, 2)] = (a[own(0, 2)] + f32(rl[b, own(0, 2)])).astype(BF)
            chain(b, 2, 0, False).start()

    def stage4(b):
        a = acc.at[b % SLOTS]

        @pl.when(z == 2)
        def _():
            chain(b, 2, 0, True).wait_recv()
            a[own(2)] += f32(rr[b, own(0)])
            sm[b, own(2)] = (a[own(3)] + f32(rr[b, own(1)])).astype(BF)
            chain(b, 1, 2 * Q, True).start()

        @pl.when(z == 1)
        def _():
            chain(b, 2, 0, False).wait_recv()
            a[own(1)] += f32(rl[b, own(1)])
            sm[b, own(2)] = (a[own(0)] + f32(rl[b, own(0)])).astype(BF)
            chain(b, 1, 2 * Q, False).start()

    def finish(b):
        a = acc.at[b % SLOTS]

        @pl.when(z == 3)
        def _():
            chain(b, 1, 2 * Q, True).wait_recv()
            a[own(3)] += f32(rr[b, own(0)])

        @pl.when(z == 0)
        def _():
            chain(b, 1, 2 * Q, False).wait_recv()
            a[own(0)] += f32(rl[b, own(0)])

        x1_load(b).wait()
        down = a[pl.ds(pl.multiple_of(z * Q, Q), Q)] + bd_ref[...]
        fin[b] = (f32(x1b[b]) + down).astype(BF)
        go_y(b, z, True).start()

        @pl.when(z < 3)
        def _():
            go_right(b, 0).start()

        @pl.when(z > 0)
        def _():
            go_left(b, 0).start()

        go_core(b, z, y, True).start()
        pltpu.make_async_copy(fin.at[b], o_ref.at[rows_of(b, z, y)], lsem).start()

    def relay(b, k):
        @pl.when(z >= k + 1)
        def _():
            go_right(b, k).wait_recv()
            if k < 2:
                @pl.when(z < 3)
                def _():
                    go_right(b, k + 1).start()
            go_y(b, (z + 3 - k) % 4).start()
            go_core(b, (z + 3 - k) % 4, y).start()

        @pl.when(z <= 2 - k)
        def _():
            go_left(b, k).wait_recv()
            if k < 2:
                @pl.when(z > 0)
                def _():
                    go_left(b, k + 1).start()
            go_y(b, (z + 1 + k) % 4).start()
            go_core(b, (z + 1 + k) % 4, y).start()

    def across(b):
        for z_ in range(4):
            go_y(b, z_).wait_recv()
            go_core(b, z_, 1 - y).start()

    stages = (multiply, stage2, stage3, stage4, finish, functools.partial(relay, k=0), functools.partial(relay, k=1), functools.partial(relay, k=2), across)

    @pl.loop(0, NB + len(stages) - 1)
    def _(t):
        for i, stage in enumerate(stages):
            b = t - i

            @pl.when((b >= 0) & (b < NB))
            def _():
                stage(b)

    def drain(sem, n):
        rows = o_ref.at[pl.ds(0, n)]
        pltpu.make_async_copy(rows, rows, sem).wait()

    n = NB * Q
    drain(dr, 8 * n)
    drain(ds, 8 * n)
    drain(ys, 4 * n)
    drain(lsem, n)
    drain(sms, 3 * n)
    ends = (z == 0) | (z == 3)

    @pl.when(ends)
    def _():
        drain(zs, n)

    @pl.when(jnp.logical_not(ends))
    def _():
        drain(zs, 5 * n)

    for b in range(NB - S1N, NB):
        swap(b).wait_send()


def down(u, w0, w1, x1, bd):
    sem = lambda n: pltpu.SemaphoreType.DMA((n,))
    one = pltpu.SemaphoreType.DMA
    return pl.pallas_call(
        down_kernel,
        out_shape=jax.ShapeDtypeStruct((3 * S, D), BF),
        in_specs=[ANY] * 4 + [pl.BlockSpec(memory_space=pltpu.VMEM)],
        out_specs=ANY,
        scratch_shapes=[
            pltpu.VMEM((2 * FF, D), BF), pltpu.VMEM((NB, BR, 2 * FF), BF), pltpu.VMEM((NB, Q, D), BF), pltpu.VMEM((BR, 512), jnp.float32),
            pltpu.VMEM((SLOTS, CH, D), jnp.float32), pltpu.VMEM((S1N, CH, D), BF), pltpu.VMEM((NB, CH, D), BF),
            pltpu.VMEM((NB, 3 * Q, D), BF), pltpu.VMEM((NB, 3 * Q, D), BF), pltpu.VMEM((NB, 3 * Q, D), BF), pltpu.VMEM((NB, Q, D), BF),
            sem(2), sem(NB), sem(NB), one, sem(S1N), sem(NB), one, sem(NB), sem(NB), one, sem(3 * NB), sem(3 * NB), one, sem(4 * NB), one, one,
        ],
        compiler_params=pltpu.CompilerParams(collective_id=0, has_side_effects=True, vmem_limit_bytes=62 * 2**20),
        cost_estimate=pl.CostEstimate(flops=4 * S * D * D, bytes_accessed=4 * D * D, transcendentals=0),
        name="down",
    )(u, w0, w1, x1, bd)


def solution(mesh):
    def local_layer(x_in, seq_lens, ln1_gain, ln1_bias, w_qkv, b_qkv, w_out, b_out, ln2_gain, ln2_bias, w_up, b_up, w_down, b_down):
        f32 = lambda v: v.astype(jnp.float32)
        wq = jnp.transpose(w_qkv, (1, 2, 3, 0)).reshape(6 * HD, D)
        bq = f32(b_qkv).reshape(6 * HD, 1)
        vec = jnp.stack([ln1_gain, ln1_bias, f32(b_out), ln2_gain, ln2_bias, f32(b_down)])
        bup = jnp.broadcast_to(f32(b_up)[None], (8, FF))
        keys, values, x1, u, down_y = front(seq_lens, x_in, vec, wq, bq, w_out.reshape(2 * HD, D), w_up, bup, w_down)
        x_out = down(u, w_down, down_y, x1, vec[5:6]).reshape(x_in.shape)
        return x_out, jnp.swapaxes(keys, 2, 3), jnp.swapaxes(values, 2, 3)

    arg_specs = (P("dp", None, None), P("dp"), P(), P(), P(None, None, "tp", None), P(None, "tp", None), P("tp", None, None), P(), P(), P(), P(None, "tp"), P("tp"), P("tp", None), P())
    cache_spec = P("dp", "tp", None, None)
    return jax.shard_map(local_layer, mesh=mesh, in_specs=arg_specs, out_specs=(P("dp", None, None), cache_spec, cache_spec), check_vma=False)
```

time: 1380 us -> 493 us (0.36)
  waiting for transfers between devices: 1060 us -> 0 us
  Pallas kernels: 0 us -> 450 us
  matrix products: 181 us -> 0 us
  other arithmetic: 122 us -> 0 us
  local copies, waits for them, and re-layouts: 1.36 us -> 33.4 us
    psum x2 -> x0, waiting for transfers between devices: 1060 us -> none  [the longest x1 535 us: local_layer(): summed_out = lax.psum(part_out, 'tp')]
    pallas_call x0 -> x2, Pallas kernels: none -> 450 us  [the longest x1 245 us: front(): pl.pallas_call(front_kernel, out_shape=(cache, cache, rows(D), rows(2 * F...]
    dot_general x5 -> x0, matrix products: 132 us -> none  [the longest x1 32.7 us: attend(): jnp.einsum('bhqs,bhsk->bhqk', attn_probs, v_all, preferred_element_type=j...]
    reduce_sum x4 -> x0, other arithmetic: 72.6 us -> none  [the longest x2 42.4 us: layer_norm(): row_mean = jnp.mean(values, axis=-1, keepdims=True)]
    sub x1 -> x0, matrix products: 49.1 us -> none  [attend(): attn_probs = jax.nn.softmax(scores, axis=-1).astype(jnp.bfloat16)]
    convert_element_type x5 -> x0, other arithmetic: 32.2 us -> none  [the longest x1 32.2 us: local_layer(): (x_mid.astype(jnp.float32) + summed_down.astype(jnp.float32) + b_down.ast...]
    unnamed x30 -> x9, local copies, waits for them, and re-layouts: 1.36 us -> 25.6 us
  transfers between devices with their start and end apart: 2 -> 0, of which waited for: 2 -> 0; matrix products, arithmetic and copies ran while one was open for 0% -> 0% of each run, Pallas kernels for 0% -> 0%
where the time goes in v1:
time: 493 us; the launch traced here: 485 us
  Pallas kernels  450 us (91%)
  local copies, waits for them, and re-layouts  33.4 us (7%)
    pallas_call x1, Pallas kernels, front(): pl.pallas_call(front_kernel, out_shape=(cache, cache, rows(D), rows(2 * F...  245 us
    pallas_call x1, Pallas kernels, down(): pl.pallas_call(down_kernel, out_shape=jax.ShapeDtypeStruct((3 * S, D), BF...  205 us
    unnamed x9, local copies, waits for them, and re-layouts  25.6 us

profile of v1, /device:TPU:0, one launch (start us, length us, event | category | flops | bytes accessed | tf_op | source)
XLA Modules:
  0.0 484.7 jit_solution(10194491111963572232)
XLA Ops:
  0.6 0.7 reshape.27.bd_ref
  1.3 0.0 copy-start.2
  1.3 0.7 stack.26
  2.1 0.7 stack.27
  2.8 0.7 reshape.26
  3.5 0.7 stack.30
  4.2 0.7 stack.31
  4.9 1.3 broadcast_in_dim.2.bup_ref
  6.2 0.7 stack.34.vec_ref
  6.9 1.5 reshape.30.bq_ref
  8.4 244.9 %front.1 = (bf16[3,2,80,2048]{3,2,1,0:T(8,128)(2,1)}, bf16[3,2,80,2048]{3,2,1,0:T(8,128)(2,1)}, bf16[3072,2560]{1,0:T(8,128)(2,1)}, bf16[3072,1280]{1,0:T(8,128)(2,1)}, bf16[640,2560]{1,0:T(8,128)(2,1)}) custom-call(s32[3]{0:T(128)} %lens_ref.1, bf16[3,2048,2560]{2,1,0:T(8,128)(2,1)} %x_ref.1, f32[6,2560]{1,0:T(8,128)} %stack.34.vec_ref, ...), custom_call_target="tpu_custom_call" | custom-call | flops 99999997952 | bytes 100000000 | tf_op jit(solution)/shard_map/front/pallas_call | solution.py:366
  253.3 0.0 copy-done.2
  253.3 205.3 %down.1 = bf16[6144,2560]{1,0:T(8,128)(2,1)} custom-call(bf16[3072,1280]{1,0:T(8,128)(2,1)} %get-tuple-element.8.u_ref, bf16[640,2560]{1,0:T(8,128)(2,1)} %w0_ref.1, bf16[640,2560]{1,0:T(8,128)(2,1)} %get-tuple-element.9.w1_ref, bf16[3072,2560]{1,0:T(8,128)(2,1)} %get-tuple-element.10.x1_ref, f32[1,2560]{1,0:T(1,128)} %copy-done.2), custom_call_target="tpu_custom_call" | custom-call | flops 53687091200 | bytes 26214400 | tf_op jit(solution)/shard_map/down/pallas_call | solution.py:618
  458.7 0.0 copy-start.1
  458.7 22.0 %copy.21 = bf16[3,2048,2560]{2,1,0:T(8,128)(2,1)} copy(bf16[3,2048,2560]{2,1,0:T(8,128)(2,1)} %bitcast.7) | data formatting | bytes 62914560
  480.7 0.0 copy-done.1
  480.7 0.0 copy-start
  480.7 1.3 copy.22
  482.0 1.0 copy-done
  483.0 1.3 copy.23
Async XLA Ops:
  1.3 252.0 %copy-start.2 = (f32[1,2560]{1,0:T(1,128)}, f32[1,2560]{1,0:T(1,128)S(1)}, u32[]{:S(2)}) copy-start(f32[1,2560]{1,0:T(1,128)S(1)} %reshape.27.bd_ref) | copy-start | bytes 30724
  458.7 22.0 %copy-start.1 = (bf16[3,2,80,2048]{3,2,1,0:T(8,128)(2,1)S(1)}, bf16[3,2,80,2048]{3,2,1,0:T(8,128)(2,1)}, u32[]{:S(2)}) copy-start(bf16[3,2,80,2048]{3,2,1,0:T(8,128)(2,1)} %get-tuple-element.11) | copy-start | bytes 5898244
  480.7 2.3 copy-start

commit v2 on v1

--- a/solution.py
+++ b/solution.py
@@ -26,14 +26,16 @@
 TB, KA, NS = 256, 96, 3
 QB = S // 4
 PER_SEQ = S // TB
-UC = 2
+UC = 4
+LAG = 4
+RING = LAG + 1
 CHUNKS = tuple((s, h) for s in range(NS) for h in range(2))
 
 
 def front_kernel(lens_ref, x_ref, vec_ref, wq_ref, bq_ref, wo_ref, wup_ref, bup_ref, wdn_ref,
                  k_out, v_out, x1_out, u_out, dn_out,
-                 wt, wu, a_all, xb, q_s, k_s, v_s, kt, a_st, bu, st1, st2,
-                 xsem, csem, osem, lsem, wsem, wos, wor, wol, woy_s, woy_r, wod_s, wod_r, ay_s, ay_r, as_, ar, al, ad_s, ad_r,
+                 wt, wu, a_all, xb, q_s, k_s, v_s, kt, a_st, bu, st1, st2, hid,
+                 xsem, csem, osem, lsem, wsem, wos, wor, wol, woy_s, woy_r, wox_s, wox_r, wod_s, wod_r, ay_s, ay_r, as_, ar, al, ad_s, ad_r,
                  b_s, b_r, yu_s, yu_r, yd_s, yd_r, xu_s, xu_r, xd_s, xd_r):
     group, me = lax.axis_index("dp"), lax.axis_index("tp")
     z, y, c = me // 4, (me // 2) % 2, me % 2
@@ -46,32 +48,42 @@
     def remote(src, dst, ss, rs, to):
         return pltpu.make_async_remote_copy(src, dst, ss, rs, device_id=to, device_id_type=MESH)
 
-    def go(copy, when=None):
+    def go(make, when=None):
         if when is None:
-            copy.start()
+            make().start()
         else:
-            @pl.when(when)
-            def _():
-                copy.start()
-        sent.append((copy, when))
+            @pl.when(when())
+            def _():
+                make().start()
+        sent.append((make, when))
 
     place = lambda z_, y_, c_: (z_ * 2 + c_) * 2 + y_
     mine = place(z, y, c)
-    wo_rows = lambda z_, y_: wt.at[pl.ds(pl.multiple_of(place(z_, y_, c) * 2 * HD, 32), 2 * HD)]
+    half = HD
+
+    def wo_part(z_, y_):
+        return wt.at[pl.ds(pl.multiple_of(place(z_, y_, c) * 2 * HD + group * half, 16), half)]
+
+    def wo_whole(z_, y_):
+        return wt.at[pl.ds(pl.multiple_of(place(z_, y_, c) * 2 * HD, 32), 2 * HD)]
+
+    def wo_mine():
+        return wo_ref.at[pl.ds(pl.multiple_of(group * half, 16), half)]
 
     def wo_line(k, to_right):
         z_ = (z + 4 - k) % 4 if to_right else (z + k) % 4
-        rows = wo_rows(z_, y)
         i = k + 3 * (not to_right)
-        return remote(wo_ref if k == 0 else rows, rows, wos.at[i], (wor if to_right else wol).at[k], right if to_right else left)
+        return remote(wo_mine() if k == 0 else wo_part(z_, y), wo_part(z_, y), wos.at[i], (wor if to_right else wol).at[k], right if to_right else left)
 
     def wo_y(z_, own=False):
-        rows = wo_rows(z_, y)
-        return remote(wo_ref if own else rows, rows, woy_s.at[z_], woy_r.at[z_], ypeer)
+        return remote(wo_mine() if own else wo_part(z_, y), wo_part(z_, y), woy_s.at[z_], woy_r.at[z_], ypeer)
+
+    def wo_x(z_, y_):
+        i = z_ + 4 * y_
+        return remote(wo_part(z_, y_), wo_part(z_, y_), wox_s.at[i], wox_r.at[i], across)
 
     def wo_core(z_, y_, own=False):
-        rows = wo_rows(z_, y_)
-        return remote(wo_ref if own else rows, rows, wod_s, wod_r, partner)
+        return remote(wo_ref if own else wo_whole(z_, y_), wo_whole(z_, y_), wod_s, wod_r, partner)
 
     def a_y(i):
         s, h = CHUNKS[i]
@@ -95,7 +107,7 @@
         return pl.ds(pl.multiple_of(group * hu + n * cu, 32), cu)
 
     def dn_rows(n):
-        return pl.ds(pl.multiple_of(group * hd + n * cd, 32), cd)
+        return pl.ds(pl.multiple_of(group * hd + n * cd, 16), cd)
 
     def yu(n):
         return remote(wup_ref.at[up_rows(n)], wu.at[1, up_rows(n)], yu_s.at[n], yu_r.at[n], ypeer)
@@ -109,7 +121,8 @@
     def xd(n):
         return remote(dn_out.at[dn_rows(n)], dn_out.at[dn_rows(n)], xd_s.at[n], xd_r.at[n], across)
 
-    bias_flow = remote(bup_ref, bu.at[1], b_s, b_r, ypeer)
+    def bias_flow():
+        return remote(bup_ref, bu.at[1], b_s, b_r, ypeer)
 
     def hop(line, k, then):
         @pl.when(z >= k + 1)
@@ -117,7 +130,7 @@
             line(k, True).wait_recv()
 
         if k < 2:
-            go(line(k + 1, True), (z >= k + 1) & (z < 3))
+            go(lambda: line(k + 1, True), lambda: (z >= k + 1) & (z < 3))
         then((z + 3 - k) % 4, z >= k + 1)
 
         @pl.when(z <= 2 - k)
@@ -125,39 +138,62 @@
             line(k, False).wait_recv()
 
         if k < 2:
-            go(line(k + 1, False), (z <= 2 - k) & (z > 0))
+            go(lambda: line(k + 1, False), lambda: (z <= 2 - k) & (z > 0))
         then((z + 1 + k) % 4, z <= 2 - k)
 
     def begin(line):
-        go(line(0, True), z < 3)
-        go(line(0, False), z > 0)
-
-    def start_if(copy, when):
+        go(lambda: line(0, True), lambda: z < 3)
+        go(lambda: line(0, False), lambda: z > 0)
+
+    def wo_then(z_, when):
         @pl.when(when)
         def _():
-            copy.start()
-
-    def wo_then(z_, when):
-        start_if(wo_y(z_), when)
-        start_if(wo_core(z_, y), when)
+            wo_y(z_).start()
+            wo_x(z_, y).start()
 
     def wo_hop(k):
         hop(wo_line, k, wo_then)
 
-    def wo_from_y():
+    def wo_from_y(k):
+        def take(z_):
+            wo_y(z_).wait_recv()
+            wo_x(z_, 1 - y).start()
+
+        if k == 0:
+            take(z)
+        else:
+            @pl.when(z >= k)
+            def _():
+                take((z + 4 - k) % 4)
+
+            @pl.when(z <= 3 - k)
+            def _():
+                take((z + k) % 4)
+
+    def wo_from_x():
         for z_ in range(4):
-            wo_y(z_).wait_recv()
+            @pl.when(z_ != z)
+            def _():
+                wo_x(z_, y).wait_recv()
+                wo_core(z_, y).start()
+        for z_ in range(4):
+            wo_x(z_, 1 - y).wait_recv()
             wo_core(z_, 1 - y).start()
 
-    def a_begin(s):
-        for i in (2 * s, 2 * s + 1):
-            a_y(i).wait_recv()
-            begin(functools.partial(a_line, i))
-            a_core(i, z).start()
-
-    def a_hop(s, k):
-        for i in (2 * s, 2 * s + 1):
-            hop(functools.partial(a_line, i), k, lambda z_, when: start_if(a_core(i, z_), when))
+    def a_send(i):
+        go(functools.partial(a_y, i))
+
+    def a_begin(i):
+        a_y(i).wait_recv()
+        begin(functools.partial(a_line, i))
+        a_core(i, z).start()
+
+    def a_hop(i, k):
+        def then(z_, when):
+            @pl.when(when)
+            def _():
+                a_core(i, z_).start()
+        hop(functools.partial(a_line, i), k, then)
 
     barrier = pltpu.get_barrier_semaphore()
     peers = (partner, ypeer, across, right, left)
@@ -168,7 +204,7 @@
         return pltpu.make_async_copy(x_ref.at[g // PER_SEQ, pl.ds(pl.multiple_of((g % PER_SEQ) * TB, TB), TB)], xb.at[g % 2], xsem.at[g % 2])
 
     x_copy(0).start()
-    locals_ = [pltpu.make_async_copy(wo_ref, wo_rows(z, y), wsem.at[0]), pltpu.make_async_copy(bup_ref, bu.at[0], wsem.at[1]), pltpu.make_async_copy(wup_ref, wu.at[0], wsem.at[2])]
+    locals_ = [pltpu.make_async_copy(wo_ref, wo_whole(z, y), wsem.at[0]), pltpu.make_async_copy(bup_ref, bu.at[0], wsem.at[1]), pltpu.make_async_copy(wup_ref, wu.at[0], wsem.at[2])]
     for copy in locals_:
         copy.start()
     row = lax.broadcasted_iota(jnp.int32, (KA - HD, S), 0)
@@ -181,27 +217,90 @@
     wo_core(z, y, True).start()
     go(bias_flow)
 
-    def qkv(s):
+    x_copy(0).wait()
+    x_copy(1).start()
+    hid[0] = ln_rows(xb[0].astype(jnp.float32), ln1_gain, ln1_bias)
+
+    def caches(s):
+        return [pltpu.make_async_copy(k_s.at[:, pl.ds(0, HD)], k_out.at[s], csem.at[0]), pltpu.make_async_copy(v_s, v_out.at[s], csem.at[1])]
+
+    def serve(table, *key):
+        for at, todo in table.items():
+            hit = functools.reduce(jnp.logical_and, [i == n for i, n in zip(key, at)])
+
+            @pl.when(hit)
+            def _():
+                todo()
+
+    def run(*todo):
+        def all_of():
+            for f, *args in todo:
+                f(*args)
+        return all_of
+
+    def send(flow, n):
+        go(functools.partial(flow, n))
+
+    def pass_on(flow, onward, n):
+        flow(n).wait_recv()
+        go(functools.partial(onward, n))
+
+    def await_all(flow):
+        for n in range(UC):
+            flow(n).wait_recv()
+
+    IN_QKV = {
+        (0, 6): run((wo_hop, 0), (wo_from_y, 0)),
+        (1, 1): run((wo_from_y, 1)),
+        (1, 4): run((wo_hop, 2), (send, yu, 0)),
+        (1, 7): run((a_begin, 0), (a_begin, 1)),
+        (2, 2): run((a_hop, 1, 0)),
+        (2, 3): run((wo_from_y, 3)),
+        (2, 4): run((a_hop, 0, 1)),
+        (2, 5): run((send, yu, 2)),
+        (2, 7): run((pass_on, yu, xu, 0)),
+    }
+    IN_ATTN = {
+        (0, 3): run((a_send, 0), (a_send, 1), (wo_hop, 1)),
+        (1, 1): run((wo_from_y, 2)),
+        (1, 3): run((a_send, 2), (a_send, 3), (send, yu, 1), (a_hop, 0, 0)),
+        (2, 0): run((a_hop, 1, 1)),
+        (2, 1): run((a_begin, 2), (a_begin, 3)),
+        (2, 2): run((a_hop, 0, 2), (pass_on, yu, xu, 1)),
+        (2, 3): run((a_send, 4), (a_send, 5), (send, yu, 3)),
+    }
+
+    @pl.loop(0, NS)
+    def _(s):
         n = lens_ref[s]
+
+        @pl.when(s > 0)
+        def _():
+            for copy in caches(s - 1):
+                copy.wait()
 
         @pl.loop(0, PER_SEQ)
         def _(b):
             g = s * PER_SEQ + b
-            x_copy(g).wait()
 
             @pl.when(g + 1 < NS * PER_SEQ)
             def _():
-                x_copy(g + 1).start()
-
-            h = ln_rows(xb[g % 2].astype(jnp.float32), ln1_gain, ln1_bias)
-            t = lax.dot_general(wq_ref[...], h, NT, preferred_element_type=jnp.float32)
-            t = (t + bq_ref[...]).astype(BF)
+                x_copy(g + 1).wait()
+
+            @pl.when(g + 2 < NS * PER_SEQ)
+            def _():
+                x_copy(g + 2).start()
+
             cols = pl.ds(pl.multiple_of(b * TB, TB), TB)
             keep = b * TB + lax.broadcasted_iota(jnp.int32, (1, TB), 1) < n
+            t = lax.dot_general(wq_ref[...], hid[g % 2], NT, preferred_element_type=jnp.float32)
+            hid[(g + 1) % 2] = ln_rows(xb[(g + 1) % 2].astype(jnp.float32), ln1_gain, ln1_bias)
+            t = (t + bq_ref[...]).astype(BF)
             for i in range(2):
                 q_s[i, :HD, cols] = t[i * HD:(i + 1) * HD]
                 k_s[i, :HD, cols] = jnp.where(keep, t[(2 + i) * HD:(3 + i) * HD], 0)
                 v_s[i, :, cols] = jnp.where(keep, t[(4 + i) * HD:(5 + i) * HD], 0)
+            serve(IN_QKV, s, b)
 
         pos = lax.broadcasted_iota(jnp.int32, (KA - HD, S), 1)
         for i in range(2):
@@ -210,10 +309,6 @@
         for copy in caches(s):
             copy.start()
 
-    def caches(s):
-        return [pltpu.make_async_copy(k_s.at[:, pl.ds(0, HD)], k_out.at[s], csem.at[0]), pltpu.make_async_copy(v_s, v_out.at[s], csem.at[1])]
-
-    def attend(s):
         causal = lax.broadcasted_iota(jnp.int32, (QB, QB), 0) <= lax.broadcasted_iota(jnp.int32, (QB, QB), 1)
 
         @pl.loop(0, 4)
@@ -242,10 +337,7 @@
             def _():
                 a_all[s, t % 2, mine] = a_st[s, t]
 
-        for copy in caches(s):
-            copy.wait()
-        go(a_y(2 * s))
-        go(a_y(2 * s + 1))
+            serve(IN_ATTN, s, t)
 
     per = QB // TB
     n_blocks = NS * 2 * per
@@ -260,96 +352,106 @@
     def put_u(i):
         return pltpu.make_async_copy(st2.at[i % 2], u_out.at[pl.ds(pl.multiple_of(i * TB, TB), TB)], lsem.at[i % 2])
 
-    def middle(i):
+    def a_ready(i):
         s, h = CHUNKS[i]
         whole = a_all.at[s, h, pl.ds(0, 8)]
         pltpu.make_async_copy(whole, whole, ad_r.at[i]).wait()
 
-        @pl.loop(i * per, (i + 1) * per)
-        def _(b):
-            res_copy(b).wait()
-
-            @pl.when(b + 1 < n_blocks)
-            def _():
-                res_copy(b + 1).start()
-
-            a = a_all[s, h, :, :, pl.ds(pl.multiple_of((b % per) * TB, TB), TB)].reshape(D, TB)
-            o = lax.dot_general(a, wt[...], TN, preferred_element_type=jnp.float32)
-            x1 = (xb[b % 2].astype(jnp.float32) + o + b_out).astype(BF)
-
-            @pl.when(b >= 2)
-            def _():
-                put_x1(b - 2).wait()
-                put_u(b - 2).wait()
-
-            st1[b % 2] = x1
-            put_x1(b).start()
-            hid = ln_rows(x1.astype(jnp.float32), ln2_gain, ln2_bias)
-            for n in range(2):
-                up = jnp.dot(hid, wu[n], preferred_element_type=jnp.float32) + bu[n, 0:1]
-                st2[b % 2, :, n * FF:(n + 1) * FF] = jnp.maximum(up, 0).astype(BF)
-            put_u(b).start()
-
-    qkv(0)
-    wo_hop(0)
-    attend(0)
-    wo_hop(1)
-    go(yu(0))
-    qkv(1)
-    a_begin(0)
-    wo_hop(2)
-    attend(1)
-    go(yu(1))
-    a_hop(0, 0)
-    wo_from_y()
-    qkv(2)
-    a_hop(0, 1)
-    a_begin(1)
-    attend(2)
+    whole = wt.at[pl.ds(0, D // 2)]
+
+    def wo_ready():
+        pltpu.make_async_copy(whole, whole, wod_r).wait()
+        bias_flow().wait_recv()
+        for copy in locals_:
+            copy.wait()
+
     res_copy(0).start()
+    run((wo_from_x,), (a_hop, 1, 2), (pass_on, yu, xu, 2), (a_hop, 2, 0), (wo_ready,))()
     for n in range(UC):
-        go(yd(n))
-    for n in range(UC):
-        yu(n).wait_recv()
-        go(xu(n))
-    a_hop(0, 2)
-    a_hop(1, 0)
-    whole = wt.at[pl.ds(0, D // 2)]
-    pltpu.make_async_copy(whole, whole, wod_r).wait()
-    bias_flow.wait_recv()
-    for copy in locals_:
-        copy.wait()
-    a_begin(2)
-    a_hop(1, 1)
-    for n in range(UC):
-        xu(n).wait_recv()
-    middle(0)
-    a_hop(2, 0)
-    a_hop(1, 2)
-    for n in range(UC):
-        yd(n).wait_recv()
-        go(xd(n))
-    middle(1)
-    a_hop(2, 1)
-    middle(2)
-    a_hop(2, 2)
-    middle(3)
-    middle(4)
-    middle(5)
-    for n in range(UC):
-        xd(n).wait_recv()
+        send(yd, n)
+
+    BEFORE = {
+        (0,): run((a_ready, 0)),
+        (1,): run((a_hop, 3, 0), (pass_on, yu, xu, 3)),
+        (2,): run((a_ready, 1), (a_hop, 2, 1)),
+        (3,): run((a_hop, 3, 1), (a_begin, 4), (a_begin, 5)),
+        (4,): run((await_all, xu), (a_hop, 2, 2), (a_ready, 2)),
+        (5,): run((a_hop, 3, 2)),
+        (6,): run((a_ready, 3), (a_hop, 4, 0), (a_hop, 5, 0)),
+        (7,): run((a_hop, 4, 1), (a_hop, 5, 1), *((pass_on, yd, xd, n) for n in range(UC))),
+        (8,): run((a_hop, 4, 2), (a_ready, 4)),
+        (9,): run((a_hop, 5, 2)),
+        (10,): run((a_ready, 5)),
+    }
+
+    def up_proj(b):
+        @pl.when(b >= 2)
+        def _():
+            put_u(b - 2).wait()
+
+        for n in range(2):
+            up = jnp.dot(hid[b % RING], wu[n], preferred_element_type=jnp.float32) + bu[n, 0:1]
+            st2[b % 2, :, n * FF:(n + 1) * FF] = jnp.maximum(up, 0).astype(BF)
+        put_u(b).start()
+
+    def out_proj(b):
+        a = a_all[b // (2 * per), (b // per) % 2, :, :, pl.ds(pl.multiple_of((b % per) * TB, TB), TB)].reshape(D, TB)
+        return lax.dot_general(a, wt[...], TN, preferred_element_type=jnp.float32)
+
+    def residual(b, o):
+        x1 = (xb[b % 2].astype(jnp.float32) + o + b_out).astype(BF)
+        st1[b % 2] = x1
+        hid[b % RING] = ln_rows(x1.astype(jnp.float32), ln2_gain, ln2_bias)
+
+    def next_rows(b):
+        res_copy(b).wait()
+
+        @pl.when(b + 1 < n_blocks)
+        def _():
+            res_copy(b + 1).start()
+
+    @pl.loop(0, n_blocks)
+    def _(b):
+        serve(BEFORE, b)
+        next_rows(b)
+
+        @pl.when(b >= 2)
+        def _():
+            put_x1(b - 2).wait()
+
+        residual(b, out_proj(b))
+        put_x1(b).start()
+
+        @pl.when((b >= LAG) & (b < 2 * LAG - 1))
+        def _():
+            up_proj(2 * (b - LAG))
+            up_proj(2 * (b - LAG) + 1)
+
+        @pl.when(b >= 2 * LAG - 1)
+        def _():
+            up_proj(b - 1)
+
+    up_proj(n_blocks - 1)
+    await_all(xd)
     for b in range(n_blocks - 2, n_blocks):
         put_x1(b).wait()
         put_u(b).wait()
-    for copy, when in sent:
+    for copy in caches(NS - 1):
+        copy.wait()
+    for make, when in sent:
         if when is None:
-            copy.wait_send()
+            make().wait_send()
         else:
-            @pl.when(when)
-            def _():
-                copy.wait_send()
+            @pl.when(when())
+            def _():
+                make().wait_send()
     for z_ in range(4):
         wo_y(z_).wait_send()
+        wo_x(z_, 1 - y).wait_send()
+
+        @pl.when(z_ != z)
+        def _():
+            wo_x(z_, y).wait_send()
     pltpu.make_async_copy(whole, whole, wod_s).wait()
     for i, (s, h) in enumerate(CHUNKS):
         pairs = a_all.at[s, h, pl.ds(0, 8)]
@@ -371,8 +473,8 @@
         scratch_shapes=[
             pltpu.VMEM((D, D), BF), pltpu.VMEM((2, D, FF), BF), pltpu.VMEM((NS, 2, 16, 2 * HD, QB), BF), pltpu.VMEM((2, TB, D), BF),
             pltpu.VMEM((2, KA, S), BF), pltpu.VMEM((2, KA, S), BF), pltpu.VMEM((2, HD, S), BF), pltpu.VMEM((2, S, KA), BF),
-            pltpu.VMEM((NS, 4, 2 * HD, QB), BF), pltpu.VMEM((2, 8, FF), jnp.float32), pltpu.VMEM((2, TB, D), BF), pltpu.VMEM((2, TB, 2 * FF), BF),
-            sem(2), sem(2), sem(2), sem(2), sem(3), sem(6), sem(3), sem(3), sem(4), sem(4), one, one, sem(nc), sem(nc), sem(6 * nc), sem(3 * nc), sem(3 * nc), sem(nc), sem(nc),
+            pltpu.VMEM((NS, 4, 2 * HD, QB), BF), pltpu.VMEM((2, 8, FF), jnp.float32), pltpu.VMEM((2, TB, D), BF), pltpu.VMEM((2, TB, 2 * FF), BF), pltpu.VMEM((RING, TB, D), BF),
+            sem(2), sem(2), sem(2), sem(2), sem(3), sem(6), sem(3), sem(3), sem(4), sem(4), sem(8), sem(8), one, one, sem(nc), sem(nc), sem(6 * nc), sem(3 * nc), sem(3 * nc), sem(nc), sem(nc),
             one, one, sem(UC), sem(UC), sem(UC), sem(UC), sem(UC), sem(UC), sem(UC), sem(UC),
         ],
         compiler_params=pltpu.CompilerParams(collective_id=1, has_side_effects=True, vmem_limit_bytes=63 * 2**20),

time: 493 us -> 444 us (0.901); the launches traced: 485 us -> 443 us
  Pallas kernels: 450 us -> 409 us
    pallas_call x1, Pallas kernels: 245 us -> 202 us  [front(): pl.pallas_call(front_kernel, out_shape=(cache, cache, rows(D), rows(2 * F...]
where the time goes in v2:
time: 444 us; the launch traced here: 443 us
  Pallas kernels  409 us (92%)
  local copies, waits for them, and re-layouts  33.4 us (8%)
    pallas_call x1, Pallas kernels, down(): pl.pallas_call(down_kernel, out_shape=jax.ShapeDtypeStruct((3 * S, D), BF...  207 us
    pallas_call x1, Pallas kernels, front(): pl.pallas_call(front_kernel, out_shape=(cache, cache, rows(D), rows(2 * F...  202 us
    unnamed x9, local copies, waits for them, and re-layouts  25.6 us

profile of v2, /device:TPU:0, one launch (start us, length us, event | category | flops | bytes accessed | tf_op | source)
XLA Modules:
  0.0 443.0 jit_solution(16535888121749945057)
XLA Ops:
  0.6 0.7 reshape.27.bd_ref
  1.3 0.0 copy-start.2
  1.3 0.7 stack.26
  2.1 0.7 stack.27
  2.8 0.7 reshape.26
  3.5 0.7 stack.30
  4.2 0.7 stack.31
  4.9 1.3 broadcast_in_dim.2.bup_ref
  6.2 0.7 stack.34.vec_ref
  6.9 1.5 reshape.30.bq_ref
  8.4 201.8 %front.1 = (bf16[3,2,80,2048]{3,2,1,0:T(8,128)(2,1)}, bf16[3,2,80,2048]{3,2,1,0:T(8,128)(2,1)}, bf16[3072,2560]{1,0:T(8,128)(2,1)}, bf16[3072,1280]{1,0:T(8,128)(2,1)}, bf16[640,2560]{1,0:T(8,128)(2,1)}) custom-call(s32[3]{0:T(128)} %lens_ref.1, bf16[3,2048,2560]{2,1,0:T(8,128)(2,1)} %x_ref.1, f32[6,2560]{1,0:T(8,128)} %stack.34.vec_ref, ...), custom_call_target="tpu_custom_call" | custom-call | flops 99999997952 | bytes 100000000 | tf_op jit(solution)/shard_map/front/pallas_call | solution.py:468
  210.2 0.0 copy-done.2
  210.3 207.2 %down.1 = bf16[6144,2560]{1,0:T(8,128)(2,1)} custom-call(bf16[3072,1280]{1,0:T(8,128)(2,1)} %get-tuple-element.8.u_ref, bf16[640,2560]{1,0:T(8,128)(2,1)} %w0_ref.1, bf16[640,2560]{1,0:T(8,128)(2,1)} %get-tuple-element.9.w1_ref, bf16[3072,2560]{1,0:T(8,128)(2,1)} %get-tuple-element.10.x1_ref, f32[1,2560]{1,0:T(1,128)} %copy-done.2), custom_call_target="tpu_custom_call" | custom-call | flops 53687091200 | bytes 26214400 | tf_op jit(solution)/shard_map/down/pallas_call | solution.py:720
  417.4 0.0 copy-start.1
  417.4 22.0 %copy.21 = bf16[3,2048,2560]{2,1,0:T(8,128)(2,1)} copy(bf16[3,2048,2560]{2,1,0:T(8,128)(2,1)} %bitcast.7) | data formatting | bytes 62914560
  439.5 0.0 copy-done.1
  439.5 0.0 copy-start
  439.5 1.3 copy.22
  440.8 1.0 copy-done
  441.7 1.3 copy.23
Async XLA Ops:
  1.3 208.9 %copy-start.2 = (f32[1,2560]{1,0:T(1,128)}, f32[1,2560]{1,0:T(1,128)S(1)}, u32[]{:S(2)}) copy-start(f32[1,2560]{1,0:T(1,128)S(1)} %reshape.27.bd_ref) | copy-start | bytes 30724
  417.4 22.0 %copy-start.1 = (bf16[3,2,80,2048]{3,2,1,0:T(8,128)(2,1)S(1)}, bf16[3,2,80,2048]{3,2,1,0:T(8,128)(2,1)}, u32[]{:S(2)}) copy-start(bf16[3,2,80,2048]{3,2,1,0:T(8,128)(2,1)} %get-tuple-element.11) | copy-start | bytes 5898244
  439.5 2.3 copy-start

commit v3 on v2

--- a/solution.py
+++ b/solution.py
@@ -29,10 +29,15 @@
 UC = 4
 LAG = 4
 RING = LAG + 1
+DOWN, UP, QKV = 5, 6, 7
+IN_QKV = {"0.6": "w0 v0", "1.1": "v1", "1.4": "w2 u0", "1.7": "b0 b1", "2.2": "h10", "2.3": "v3", "2.4": "h01", "2.5": "u2", "2.7": "p0"}
+IN_ATTN = {"0.3": "s0 s1 w1", "1.1": "v2", "1.3": "s2 s3 u1 h00", "2.0": "h11", "2.1": "b2 b3", "2.2": "h02 p1", "2.3": "s4 s5 u3"}
+AFTER = "x h12 p2 h20 o"
+BEFORE = {"0": "r0", "1": "h30 p3", "2": "r1 h21", "3": "h31 b4", "4": "q h22 r2", "5": "h32 h40 b5", "6": "r3 h41", "7": "h50 h42 d", "8": "r4 h51", "9": "h52", "10": "r5"}
 CHUNKS = tuple((s, h) for s in range(NS) for h in range(2))
 
 
-def front_kernel(lens_ref, x_ref, vec_ref, wq_ref, bq_ref, wo_ref, wup_ref, bup_ref, wdn_ref,
+def front_kernel(lens_ref, x_ref, vec_ref, wq_ref, wo_ref, wup_ref, wdn_ref,
                  k_out, v_out, x1_out, u_out, dn_out,
                  wt, wu, a_all, xb, q_s, k_s, v_s, kt, a_st, bu, st1, st2, hid,
                  xsem, csem, osem, lsem, wsem, wos, wor, wol, woy_s, woy_r, wox_s, wox_r, wod_s, wod_r, ay_s, ay_r, as_, ar, al, ad_s, ad_r,
@@ -43,6 +48,7 @@
     partner, ypeer, across = dev(z, y, 1 - c), dev(z, 1 - y, c), (1 - group, me)
     right, left = dev((z + 1) % 4, y, c), dev((z + 3) % 4, y, c)
     ln1_gain, ln1_bias, b_out, ln2_gain, ln2_bias = (vec_ref[i:i + 1] for i in range(5))
+    b_qkv = vec_ref[:, :512].T[:6 * HD, QKV:QKV + 1]
     sent = []
 
     def remote(src, dst, ss, rs, to):
@@ -122,7 +128,7 @@
         return remote(dn_out.at[dn_rows(n)], dn_out.at[dn_rows(n)], xd_s.at[n], xd_r.at[n], across)
 
     def bias_flow():
-        return remote(bup_ref, bu.at[1], b_s, b_r, ypeer)
+        return remote(vec_ref.at[:, pl.ds(0, FF)], bu, b_s, b_r, ypeer)
 
     def hop(line, k, then):
         @pl.when(z >= k + 1)
@@ -204,7 +210,7 @@
         return pltpu.make_async_copy(x_ref.at[g // PER_SEQ, pl.ds(pl.multiple_of((g % PER_SEQ) * TB, TB), TB)], xb.at[g % 2], xsem.at[g % 2])
 
     x_copy(0).start()
-    locals_ = [pltpu.make_async_copy(wo_ref, wo_whole(z, y), wsem.at[0]), pltpu.make_async_copy(bup_ref, bu.at[0], wsem.at[1]), pltpu.make_async_copy(wup_ref, wu.at[0], wsem.at[2])]
+    locals_ = [pltpu.make_async_copy(wo_ref, wo_whole(z, y), wsem.at[0]), pltpu.make_async_copy(wup_ref, wu.at[0], wsem.at[1])]
     for copy in locals_:
         copy.start()
     row = lax.broadcasted_iota(jnp.int32, (KA - HD, S), 0)
@@ -224,20 +230,6 @@
     def caches(s):
         return [pltpu.make_async_copy(k_s.at[:, pl.ds(0, HD)], k_out.at[s], csem.at[0]), pltpu.make_async_copy(v_s, v_out.at[s], csem.at[1])]
 
-    def serve(table, *key):
-        for at, todo in table.items():
-            hit = functools.reduce(jnp.logical_and, [i == n for i, n in zip(key, at)])
-
-            @pl.when(hit)
-            def _():
-                todo()
-
-    def run(*todo):
-        def all_of():
-            for f, *args in todo:
-                f(*args)
-        return all_of
-
     def send(flow, n):
         go(functools.partial(flow, n))
 
@@ -249,26 +241,39 @@
         for n in range(UC):
             flow(n).wait_recv()
 
-    IN_QKV = {
-        (0, 6): run((wo_hop, 0), (wo_from_y, 0)),
-        (1, 1): run((wo_from_y, 1)),
-        (1, 4): run((wo_hop, 2), (send, yu, 0)),
-        (1, 7): run((a_begin, 0), (a_begin, 1)),
-        (2, 2): run((a_hop, 1, 0)),
-        (2, 3): run((wo_from_y, 3)),
-        (2, 4): run((a_hop, 0, 1)),
-        (2, 5): run((send, yu, 2)),
-        (2, 7): run((pass_on, yu, xu, 0)),
+    whole = wt.at[pl.ds(0, D // 2)]
+
+    def wo_ready():
+        pltpu.make_async_copy(whole, whole, wod_r).wait()
+        bias_flow().wait_recv()
+        for copy in locals_:
+            copy.wait()
+
+    def a_ready(i):
+        s, h = CHUNKS[i]
+        pairs = a_all.at[s, h, pl.ds(0, 8)]
+        pltpu.make_async_copy(pairs, pairs, ad_r.at[i]).wait()
+
+    def down_over():
+        for n in range(UC):
+            pass_on(yd, xd, n)
+
+    todo = {
+        "w": wo_hop, "v": wo_from_y, "x": wo_from_x, "o": wo_ready,
+        "s": a_send, "b": a_begin, "h": a_hop, "r": a_ready,
+        "u": functools.partial(send, yu), "p": functools.partial(pass_on, yu, xu), "q": functools.partial(await_all, xu),
+        "d": down_over,
     }
-    IN_ATTN = {
-        (0, 3): run((a_send, 0), (a_send, 1), (wo_hop, 1)),
-        (1, 1): run((wo_from_y, 2)),
-        (1, 3): run((a_send, 2), (a_send, 3), (send, yu, 1), (a_hop, 0, 0)),
-        (2, 0): run((a_hop, 1, 1)),
-        (2, 1): run((a_begin, 2), (a_begin, 3)),
-        (2, 2): run((a_hop, 0, 2), (pass_on, yu, xu, 1)),
-        (2, 3): run((a_send, 4), (a_send, 5), (send, yu, 3)),
-    }
+
+    def run(words):
+        for w in words.split():
+            todo[w[0]](*map(int, w[1:]))
+
+    def serve(table, *key):
+        for at, words in table.items():
+            @pl.when(functools.reduce(jnp.logical_and, [i == int(n) for i, n in zip(key, at.split("."))]))
+            def _():
+                run(words)
 
     @pl.loop(0, NS)
     def _(s):
@@ -295,7 +300,7 @@
             keep = b * TB + lax.broadcasted_iota(jnp.int32, (1, TB), 1) < n
             t = lax.dot_general(wq_ref[...], hid[g % 2], NT, preferred_element_type=jnp.float32)
             hid[(g + 1) % 2] = ln_rows(xb[(g + 1) % 2].astype(jnp.float32), ln1_gain, ln1_bias)
-            t = (t + bq_ref[...]).astype(BF)
+            t = (t + b_qkv).astype(BF)
             for i in range(2):
                 q_s[i, :HD, cols] = t[i * HD:(i + 1) * HD]
                 k_s[i, :HD, cols] = jnp.where(keep, t[(2 + i) * HD:(3 + i) * HD], 0)
@@ -352,45 +357,18 @@
     def put_u(i):
         return pltpu.make_async_copy(st2.at[i % 2], u_out.at[pl.ds(pl.multiple_of(i * TB, TB), TB)], lsem.at[i % 2])
 
-    def a_ready(i):
-        s, h = CHUNKS[i]
-        whole = a_all.at[s, h, pl.ds(0, 8)]
-        pltpu.make_async_copy(whole, whole, ad_r.at[i]).wait()
-
-    whole = wt.at[pl.ds(0, D // 2)]
-
-    def wo_ready():
-        pltpu.make_async_copy(whole, whole, wod_r).wait()
-        bias_flow().wait_recv()
-        for copy in locals_:
-            copy.wait()
-
     res_copy(0).start()
-    run((wo_from_x,), (a_hop, 1, 2), (pass_on, yu, xu, 2), (a_hop, 2, 0), (wo_ready,))()
+    run(AFTER)
     for n in range(UC):
         send(yd, n)
 
-    BEFORE = {
-        (0,): run((a_ready, 0)),
-        (1,): run((a_hop, 3, 0), (pass_on, yu, xu, 3)),
-        (2,): run((a_ready, 1), (a_hop, 2, 1)),
-        (3,): run((a_hop, 3, 1), (a_begin, 4), (a_begin, 5)),
-        (4,): run((await_all, xu), (a_hop, 2, 2), (a_ready, 2)),
-        (5,): run((a_hop, 3, 2)),
-        (6,): run((a_ready, 3), (a_hop, 4, 0), (a_hop, 5, 0)),
-        (7,): run((a_hop, 4, 1), (a_hop, 5, 1), *((pass_on, yd, xd, n) for n in range(UC))),
-        (8,): run((a_hop, 4, 2), (a_ready, 4)),
-        (9,): run((a_hop, 5, 2)),
-        (10,): run((a_ready, 5)),
-    }
-
     def up_proj(b):
         @pl.when(b >= 2)
         def _():
             put_u(b - 2).wait()
 
         for n in range(2):
-            up = jnp.dot(hid[b % RING], wu[n], preferred_element_type=jnp.float32) + bu[n, 0:1]
+            up = jnp.dot(hid[b % RING], wu[n], preferred_element_type=jnp.float32) + (bu if n else vec_ref)[UP:UP + 1, :FF]
             st2[b % 2, :, n * FF:(n + 1) * FF] = jnp.maximum(up, 0).astype(BF)
         put_u(b).start()
 
@@ -458,7 +436,7 @@
         pltpu.make_async_copy(pairs, pairs, ad_s.at[i]).wait()
 
 
-def front(lens, x, vec, wq, bq, wo, wup, bup, wdn):
+def front(lens, x, vec, wq, wo, wup, wdn):
     v = pl.BlockSpec(memory_space=pltpu.VMEM)
     sem = lambda n: pltpu.SemaphoreType.DMA((n,))
     one = pltpu.SemaphoreType.DMA
@@ -468,19 +446,19 @@
     return pl.pallas_call(
         front_kernel,
         out_shape=(cache, cache, rows(D), rows(2 * FF), jax.ShapeDtypeStruct((FF, D), BF)),
-        in_specs=[pl.BlockSpec(memory_space=pltpu.SMEM), ANY, v, v, v, ANY, ANY, ANY, ANY],
+        in_specs=[pl.BlockSpec(memory_space=pltpu.SMEM), ANY, v, v, ANY, ANY, ANY],
         out_specs=(ANY,) * 5,
         scratch_shapes=[
             pltpu.VMEM((D, D), BF), pltpu.VMEM((2, D, FF), BF), pltpu.VMEM((NS, 2, 16, 2 * HD, QB), BF), pltpu.VMEM((2, TB, D), BF),
             pltpu.VMEM((2, KA, S), BF), pltpu.VMEM((2, KA, S), BF), pltpu.VMEM((2, HD, S), BF), pltpu.VMEM((2, S, KA), BF),
-            pltpu.VMEM((NS, 4, 2 * HD, QB), BF), pltpu.VMEM((2, 8, FF), jnp.float32), pltpu.VMEM((2, TB, D), BF), pltpu.VMEM((2, TB, 2 * FF), BF), pltpu.VMEM((RING, TB, D), BF),
-            sem(2), sem(2), sem(2), sem(2), sem(3), sem(6), sem(3), sem(3), sem(4), sem(4), sem(8), sem(8), one, one, sem(nc), sem(nc), sem(6 * nc), sem(3 * nc), sem(3 * nc), sem(nc), sem(nc),
+            pltpu.VMEM((NS, 4, 2 * HD, QB), BF), pltpu.VMEM((8, FF), jnp.float32), pltpu.VMEM((2, TB, D), BF), pltpu.VMEM((2, TB, 2 * FF), BF), pltpu.VMEM((RING, TB, D), BF),
+            sem(2), sem(2), sem(2), sem(2), sem(2), sem(6), sem(3), sem(3), sem(4), sem(4), sem(8), sem(8), one, one, sem(nc), sem(nc), sem(6 * nc), sem(3 * nc), sem(3 * nc), sem(nc), sem(nc),
             one, one, sem(UC), sem(UC), sem(UC), sem(UC), sem(UC), sem(UC), sem(UC), sem(UC),
         ],
         compiler_params=pltpu.CompilerParams(collective_id=1, has_side_effects=True, vmem_limit_bytes=63 * 2**20),
         cost_estimate=pl.CostEstimate(flops=10**11, bytes_accessed=10**8, transcendentals=0),
         name="front",
-    )(lens, x, vec, wq, bq, wo, wup, bup, wdn)
+    )(lens, x, vec, wq, wo, wup, wdn)
 
 
 BR = 128
@@ -576,69 +554,38 @@
     def own(i, n=1):
         return slice(i * Q, (i + n) * Q)
 
+    def pass_sums(b, n):
+        a = acc.at[b % SLOTS]
+        at = 0 if n >= 3 else 2 * Q
+        for to_right in (True, False):
+            @pl.when(z == (4 - n if to_right else n - 1))
+            def _():
+                first = (4 - n) * to_right
+                keep = 0 if to_right else n - 1
+                rest = first + to_right
+                if n < 4:
+                    chain(b, n, 0, to_right).wait_recv()
+                    got = rr if to_right else rl
+                    a[own(first + keep)] += f32(got[b, own(keep)])
+                    if n > 1:
+                        sm[b, pl.ds(at, (n - 1) * Q)] = (a[own(rest, n - 1)] + f32(got[b, own(to_right, n - 1)])).astype(BF)
+                else:
+                    sm[b] = a[own(rest, n - 1)].astype(BF)
+                if n > 1:
+                    chain(b, n - 1, at, to_right).start()
+
     def stage2(b):
         swap(b).wait_recv()
         acc[b % SLOTS] += f32(r1[b])
-
-        @pl.when(z == 0)
-        def _():
-            sm[b] = acc[b % SLOTS, own(1, 3)].astype(BF)
-            chain(b, 3, 0, True).start()
-
-        @pl.when(z == 3)
-        def _():
-            sm[b] = acc[b % SLOTS, own(0, 3)].astype(BF)
-            chain(b, 3, 0, False).start()
-
-    def stage3(b):
+        pass_sums(b, 4)
+
+    stage3, stage4 = functools.partial(pass_sums, n=3), functools.partial(pass_sums, n=2)
+
+    def finish(b):
+        pass_sums(b, 1)
         a = acc.at[b % SLOTS]
-
-        @pl.when(z == 1)
-        def _():
-            chain(b, 3, 0, True).wait_recv()
-            a[own(1)] += f32(rr[b, own(0)])
-            sm[b, own(0, 2)] = (a[own(2, 2)] + f32(rr[b, own(1, 2)])).astype(BF)
-            chain(b, 2, 0, True).start()
-
-        @pl.when(z == 2)
-        def _():
-            chain(b, 3, 0, False).wait_recv()
-            a[own(2)] += f32(rl[b, own(2)])
-            sm[b, own(0, 2)] = (a[own(0, 2)] + f32(rl[b, own(0, 2)])).astype(BF)
-            chain(b, 2, 0, False).start()
-
-    def stage4(b):
-        a = acc.at[b % SLOTS]
-
-        @pl.when(z == 2)
-        def _():
-            chain(b, 2, 0, True).wait_recv()
-            a[own(2)] += f32(rr[b, own(0)])
-            sm[b, own(2)] = (a[own(3)] + f32(rr[b, own(1)])).astype(BF)
-            chain(b, 1, 2 * Q, True).start()
-
-        @pl.when(z == 1)
-        def _():
-            chain(b, 2, 0, False).wait_recv()
-            a[own(1)] += f32(rl[b, own(1)])
-            sm[b, own(2)] = (a[own(0)] + f32(rl[b, own(0)])).astype(BF)
-            chain(b, 1, 2 * Q, False).start()
-
-    def finish(b):
-        a = acc.at[b % SLOTS]
-
-        @pl.when(z == 3)
-        def _():
-            chain(b, 1, 2 * Q, True).wait_recv()
-            a[own(3)] += f32(rr[b, own(0)])
-
-        @pl.when(z == 0)
-        def _():
-            chain(b, 1, 2 * Q, False).wait_recv()
-            a[own(0)] += f32(rl[b, own(0)])
-
         x1_load(b).wait()
-        down = a[pl.ds(pl.multiple_of(z * Q, Q), Q)] + bd_ref[...]
+        down = a[pl.ds(pl.multiple_of(z * Q, Q), Q)] + bd_ref[DOWN:DOWN + 1]
         fin[b] = (f32(x1b[b]) + down).astype(BF)
         go_y(b, z, True).start()
 
@@ -738,11 +685,10 @@
     def local_layer(x_in, seq_lens, ln1_gain, ln1_bias, w_qkv, b_qkv, w_out, b_out, ln2_gain, ln2_bias, w_up, b_up, w_down, b_down):
         f32 = lambda v: v.astype(jnp.float32)
         wq = jnp.transpose(w_qkv, (1, 2, 3, 0)).reshape(6 * HD, D)
-        bq = f32(b_qkv).reshape(6 * HD, 1)
-        vec = jnp.stack([ln1_gain, ln1_bias, f32(b_out), ln2_gain, ln2_bias, f32(b_down)])
-        bup = jnp.broadcast_to(f32(b_up)[None], (8, FF))
-        keys, values, x1, u, down_y = front(seq_lens, x_in, vec, wq, bq, w_out.reshape(2 * HD, D), w_up, bup, w_down)
-        x_out = down(u, w_down, down_y, x1, vec[5:6]).reshape(x_in.shape)
+        wide = lambda v: jnp.pad(f32(v).reshape(-1), (0, D - v.size))
+        vec = jnp.stack([wide(v) for v in (ln1_gain, ln1_bias, b_out, ln2_gain, ln2_bias, b_down, b_up, b_qkv)])
+        keys, values, x1, u, down_y = front(seq_lens, x_in, vec, wq, w_out.reshape(2 * HD, D), w_up, w_down)
+        x_out = down(u, w_down, down_y, x1, vec).reshape(x_in.shape)
         return x_out, jnp.swapaxes(keys, 2, 3), jnp.swapaxes(values, 2, 3)
 
     arg_specs = (P("dp", None, None), P("dp"), P(), P(), P(None, None, "tp", None), P(None, "tp", None), P("tp", None, None), P(), P(), P(), P(None, "tp"), P("tp"), P("tp", None), P())

time: 444 us -> 441 us (level)
    unnamed x9 -> x7, local copies, waits for them, and re-layouts: 25.6 us -> 25.6 us
where the time goes in v3:
time: 441 us; the launch traced here: 440 us
  Pallas kernels  408 us (93%)
  local copies, waits for them, and re-layouts  31.4 us (7%)
    pallas_call x1, Pallas kernels, down(): pl.pallas_call(down_kernel, out_shape=jax.ShapeDtypeStruct((3 * S, D), BF...  206 us
    pallas_call x1, Pallas kernels, front(): pl.pallas_call(front_kernel, out_shape=(cache, cache, rows(D), rows(2 * F...  202 us
    unnamed x7, local copies, waits for them, and re-layouts  25.6 us

profile of v3, /device:TPU:0, one launch (start us, length us, event | category | flops | bytes accessed | tf_op | source)
XLA Modules:
  0.0 440.4 jit_solution(17685200757007430016)
XLA Ops:
  0.6 0.8 reshape.19
  1.4 0.7 stack.39
  2.1 0.7 stack.40
  2.8 0.7 reshape.23
  3.5 0.7 stack.43
  4.2 0.7 stack.44
  5.0 0.7 reshape.24
  5.7 0.7 pad_convert_fusion.1
  6.4 0.8 stack.51.vec_ref.bd_ref
  7.1 202.1 %front.1 = (bf16[3,2,80,2048]{3,2,1,0:T(8,128)(2,1)}, bf16[3,2,80,2048]{3,2,1,0:T(8,128)(2,1)}, bf16[3072,2560]{1,0:T(8,128)(2,1)}, bf16[3072,1280]{1,0:T(8,128)(2,1)}, bf16[640,2560]{1,0:T(8,128)(2,1)}) custom-call(s32[3]{0:T(128)} %lens_ref.1, bf16[3,2048,2560]{2,1,0:T(8,128)(2,1)} %x_ref.1, f32[8,2560]{1,0:T(8,128)} %stack.51.vec_ref.bd_ref, ...), custom_call_target="tpu_custom_call" | custom-call | flops 99999997952 | bytes 100000000 | tf_op jit(solution)/shard_map/front/pallas_call | solution.py:446
  209.3 205.5 %down.1 = bf16[6144,2560]{1,0:T(8,128)(2,1)} custom-call(bf16[3072,1280]{1,0:T(8,128)(2,1)} %get-tuple-element.8.u_ref, bf16[640,2560]{1,0:T(8,128)(2,1)} %w0_ref.1, bf16[640,2560]{1,0:T(8,128)(2,1)} %get-tuple-element.9.w1_ref, bf16[3072,2560]{1,0:T(8,128)(2,1)} %get-tuple-element.10.x1_ref, f32[8,2560]{1,0:T(8,128)} %stack.51.vec_ref.bd_ref), custom_call_target="tpu_custom_call" | custom-call | flops 53687091200 | bytes 26214400 | tf_op jit(solution)/shard_map/down/pallas_call | solution.py:667
  414.8 0.0 copy-start.1
  414.8 22.0 %copy.20 = bf16[3,2048,2560]{2,1,0:T(8,128)(2,1)} copy(bf16[3,2048,2560]{2,1,0:T(8,128)(2,1)} %bitcast.7) | data formatting | bytes 62914560
  436.9 0.0 copy-done.1
  436.9 0.0 copy-start
  436.9 1.3 copy.21
  438.1 1.0 copy-done
  439.1 1.3 copy.22
  (3 shorter events, 0.0 us)
Async XLA Ops:
  414.8 22.0 %copy-start.1 = (bf16[3,2,80,2048]{3,2,1,0:T(8,128)(2,1)S(1)}, bf16[3,2,80,2048]{3,2,1,0:T(8,128)(2,1)}, u32[]{:S(2)}) copy-start(bf16[3,2,80,2048]{3,2,1,0:T(8,128)(2,1)} %get-tuple-element.11) | copy-start | bytes 5898244
  436.9 2.3 copy-start

commit v4 on v3

--- a/solution.py
+++ b/solution.py
@@ -1,3 +1,4 @@
+import collections
 import functools
 
 import jax
@@ -32,7 +33,7 @@
 DOWN, UP, QKV = 5, 6, 7
 IN_QKV = {"0.6": "w0 v0", "1.1": "v1", "1.4": "w2 u0", "1.7": "b0 b1", "2.2": "h10", "2.3": "v3", "2.4": "h01", "2.5": "u2", "2.7": "p0"}
 IN_ATTN = {"0.3": "s0 s1 w1", "1.1": "v2", "1.3": "s2 s3 u1 h00", "2.0": "h11", "2.1": "b2 b3", "2.2": "h02 p1", "2.3": "s4 s5 u3"}
-AFTER = "x h12 p2 h20 o"
+AFTER = ("x h12 p2", "h20 o")
 BEFORE = {"0": "r0", "1": "h30 p3", "2": "r1 h21", "3": "h31 b4", "4": "q h22 r2", "5": "h32 h40 b5", "6": "r3 h41", "7": "h50 h42 d", "8": "r4 h51", "9": "h52", "10": "r5"}
 CHUNKS = tuple((s, h) for s in range(NS) for h in range(2))
 
@@ -358,7 +359,8 @@
         return pltpu.make_async_copy(st2.at[i % 2], u_out.at[pl.ds(pl.multiple_of(i * TB, TB), TB)], lsem.at[i % 2])
 
     res_copy(0).start()
-    run(AFTER)
+    for words in AFTER:
+        run(words)
     for n in range(UC):
         send(yd, n)
 

time: 441 us -> 441 us (level)
  no operation moved by 1% of the time
where the time goes in v4:
time: 441 us; the launch traced here: 440 us
  Pallas kernels  408 us (93%)
  local copies, waits for them, and re-layouts  31.4 us (7%)
    pallas_call x1, Pallas kernels, down(): pl.pallas_call(down_kernel, out_shape=jax.ShapeDtypeStruct((3 * S, D), BF...  206 us
    pallas_call x1, Pallas kernels, front(): pl.pallas_call(front_kernel, out_shape=(cache, cache, rows(D), rows(2 * F...  202 us
    unnamed x7, local copies, waits for them, and re-layouts  25.6 us

profile of v4, /device:TPU:0, one launch (start us, length us, event | category | flops | bytes accessed | tf_op | source)
XLA Modules:
  0.0 440.4 jit_solution(17685200757007430016)
XLA Ops:
  0.6 0.8 reshape.19
  1.4 0.7 stack.39
  2.1 0.7 stack.40
  2.8 0.7 reshape.23
  3.5 0.7 stack.43
  4.2 0.7 stack.44
  5.0 0.7 reshape.24
  5.7 0.7 pad_convert_fusion.1
  6.4 0.8 stack.51.vec_ref.bd_ref
  7.1 202.1 %front.1 = (bf16[3,2,80,2048]{3,2,1,0:T(8,128)(2,1)}, bf16[3,2,80,2048]{3,2,1,0:T(8,128)(2,1)}, bf16[3072,2560]{1,0:T(8,128)(2,1)}, bf16[3072,1280]{1,0:T(8,128)(2,1)}, bf16[640,2560]{1,0:T(8,128)(2,1)}) custom-call(s32[3]{0:T(128)} %lens_ref.1, bf16[3,2048,2560]{2,1,0:T(8,128)(2,1)} %x_ref.1, f32[8,2560]{1,0:T(8,128)} %stack.51.vec_ref.bd_ref, ...), custom_call_target="tpu_custom_call" | custom-call | flops 99999997952 | bytes 100000000 | tf_op jit(solution)/shard_map/front/pallas_call | solution.py:448
  209.3 205.5 %down.1 = bf16[6144,2560]{1,0:T(8,128)(2,1)} custom-call(bf16[3072,1280]{1,0:T(8,128)(2,1)} %get-tuple-element.8.u_ref, bf16[640,2560]{1,0:T(8,128)(2,1)} %w0_ref.1, bf16[640,2560]{1,0:T(8,128)(2,1)} %get-tuple-element.9.w1_ref, bf16[3072,2560]{1,0:T(8,128)(2,1)} %get-tuple-element.10.x1_ref, f32[8,2560]{1,0:T(8,128)} %stack.51.vec_ref.bd_ref), custom_call_target="tpu_custom_call" | custom-call | flops 53687091200 | bytes 26214400 | tf_op jit(solution)/shard_map/down/pallas_call | solution.py:669
  414.8 0.0 copy-start.1
  414.8 22.0 %copy.20 = bf16[3,2048,2560]{2,1,0:T(8,128)(2,1)} copy(bf16[3,2048,2560]{2,1,0:T(8,128)(2,1)} %bitcast.7) | data formatting | bytes 62914560
  436.9 0.0 copy-done.1
  436.9 0.0 copy-start
  436.9 1.3 copy.21
  438.1 1.0 copy-done
  439.1 1.3 copy.22
  (3 shorter events, 0.0 us)
Async XLA Ops:
  414.8 22.0 %copy-start.1 = (bf16[3,2,80,2048]{3,2,1,0:T(8,128)(2,1)S(1)}, bf16[3,2,80,2048]{3,2,1,0:T(8,128)(2,1)}, u32[]{:S(2)}) copy-start(bf16[3,2,80,2048]{3,2,1,0:T(8,128)(2,1)} %get-tuple-element.11) | copy-start | bytes 5898244
  436.9 2.3 copy-start
